TPU v7x, 32 devices: a whole 2x2x4 slice. The times are simulated.
32 devices in a mesh: ctx: 8 (over z, x), head: 4 (over y, core).
Axes of the slice: x: 2, y: 2, z: 4, core: 2. Of those that a mesh axis runs over, the one named last changes fastest.
Arguments:
- queries: bfloat16 [4096, 4096], P('ctx', 'head'), may hold values from -5 to 5
- key_rows: bfloat16 [4096, 1024], P('ctx', 'head'), may hold values from -5 to 5
- value_rows: bfloat16 [4096, 1024], P('ctx', 'head'), may hold values from -6 to 6
- slash_offsets: int32 [32, 4], P('head'), may hold values from 0 to 8, as said below
- union_blocks: int32 [8, 8, 2], P('head'), may hold values from 0 to 7, as said below
- head_picks: int32 [32, 8, 1], P('head'), may hold values from 0 to 1, as said below
- owner_counts: int32 [32, 8], P('head'), may hold values from 0 to 1, as said below
- out_weight: bfloat16 [4096, 4096], P(None, 'head'), may hold values from -0.09375 to 0.09375
Outputs:
- projected: bfloat16 [4096, 4096], P('ctx', 'head')
Inputs may be any that keep to these rules, and one draw needn't show every extreme that they name: `slash_offsets`: each head's offsets are distinct and include 0 and 8. `union_blocks`: the 2 entries of each KV head and sequence block are distinct. `head_picks`: the 1 entries of each query head and sequence block are distinct. `owner_counts`: equal to 1 for sequence block 0.
All inputs are finite; a program needn't handle non-finite values.
Results may differ from a plain program's by a relative error of at most 0.0056.
Values may be sent and summed in bfloat16 or wider, within the bound.
No kernel may reach another device: no remote copies, remote signals or barrier semaphores. Data moves between devices by JAX's collectives and lax.ppermute only.
A program may use at most 128 MiB of HBM per device.

v0:
```python
import jax
import jax.numpy as jnp
from jax import lax
from jax.sharding import PartitionSpec as P

HEAD_SIZE = 128
BLOCK_TOKENS = 64
NS = 4
VPER = 1
UNION = 2


def from_behind(array, axis, by):
    length = lax.axis_size(axis)
    pairs = [(i, i + by) for i in range(length) if 0 <= i + by < length]
    return lax.ppermute(array, axis, pairs)


def attend(
    vert_scores, vert_mask, diagonal_scores, slash_mask, vert_values, diagonal_values, per_dev
):
    masked_vert = jnp.where(vert_mask, vert_scores, -1e30)
    masked_slash = jnp.where(slash_mask, diagonal_scores, -1e30)
    peak = jnp.maximum(
        jnp.max(masked_vert, axis=-1, keepdims=True), jnp.max(masked_slash, axis=-1, keepdims=True)
    )
    weight_vert = jnp.exp(masked_vert - peak)
    weight_slash = jnp.exp(masked_slash - peak)
    total = jnp.sum(weight_vert, axis=-1, keepdims=True) + jnp.sum(
        weight_slash, axis=-1, keepdims=True
    )
    prob_vert = weight_vert.astype(jnp.bfloat16)
    slash_probability = weight_slash.astype(jnp.bfloat16).reshape(
        per_dev, BLOCK_TOKENS, NS, BLOCK_TOKENS
    )
    numer = jnp.dot(prob_vert, vert_values, preferred_element_type=jnp.float32)
    diagonal_portion = jnp.einsum(
        "wojf,wjfl->wol", slash_probability, diagonal_values, preferred_element_type=jnp.float32
    )
    numer = numer + diagonal_portion.reshape(per_dev * BLOCK_TOKENS, HEAD_SIZE)
    return (numer / total).astype(jnp.bfloat16)


def shards(
    queries, key_rows, value_rows, slash_offsets, union_blocks, head_picks, owner_counts, out_weight
):
    tokens = queries.shape[0]
    per_dev = tokens // BLOCK_TOKENS
    heads_here = slash_offsets.shape[0]
    groups_here = key_rows.shape[1] // HEAD_SIZE
    group_size = heads_here // groups_here
    owners = lax.axis_size("ctx")
    device_rank = lax.axis_index("ctx")
    scale_of_scores = jnp.float32(HEAD_SIZE ** (-0.5))
    stacked = jnp.stack([key_rows, value_rows])
    previous = from_behind(stacked, "ctx", 1)
    extended = jnp.concatenate([previous, stacked], axis=1).reshape(
        2, 2 * per_dev, BLOCK_TOKENS, groups_here, HEAD_SIZE
    )
    local_blocks = stacked.reshape(2, per_dev, BLOCK_TOKENS, groups_here, HEAD_SIZE)
    head_group = jnp.arange(heads_here, dtype=jnp.int32) // group_size
    mine_union = lax.dynamic_index_in_dim(union_blocks, device_rank, 1, keepdims=False)
    owner_base = jnp.arange(owners, dtype=jnp.int32)[:, None] * per_dev
    slot_rank = jnp.arange(VPER, dtype=jnp.int32)
    chosen = slot_rank[None, None, :] < owner_counts[:, :, None]
    block_rows = local_blocks[
        :, mine_union, :, jnp.arange(groups_here, dtype=jnp.int32)[:, None], :
    ]
    gathered = lax.all_gather(block_rows[:, None], "ctx", axis=1, tiled=True)
    matches = head_picks[:, :, :, None] == jnp.arange(UNION, dtype=jnp.int32)[None, None, None, :]
    slot_valid = jnp.any(matches & chosen[:, :, :, None], axis=2)
    slot_block = owner_base[None] + union_blocks[head_group]
    source_of = [head_index // group_size for head_index in range(heads_here)]
    query_place = device_rank * tokens + jnp.arange(tokens, dtype=jnp.int32)
    query_block = device_rank * per_dev + jnp.arange(per_dev, dtype=jnp.int32)
    inner_offset = jnp.arange(BLOCK_TOKENS, dtype=jnp.int32)
    local_index = jnp.arange(per_dev, dtype=jnp.int32)
    per_head = []
    for head_index in range(heads_here):
        kv_index = head_index // group_size
        offsets = slash_offsets[head_index]
        query_head = queries[:, head_index * HEAD_SIZE : (head_index + 1) * HEAD_SIZE]
        vertical = gathered[source_of[head_index]]
        blocks_flat = slot_block[head_index].reshape(-1)
        valid_flat = slot_valid[head_index].reshape(-1)
        slot_count = blocks_flat.shape[0]
        vert_keys = vertical[:, :, 0].reshape(slot_count * BLOCK_TOKENS, HEAD_SIZE)
        vert_values = vertical[:, :, 1].reshape(slot_count * BLOCK_TOKENS, HEAD_SIZE)
        vert_scores = (
            jnp.einsum("qd,kd->qk", query_head, vert_keys, preferred_element_type=jnp.float32)
            * scale_of_scores
        )
        distance = query_block[:, None] - blocks_flat[None, :]
        on_slash = jnp.any(distance[:, :, None] == offsets[None, None, :], axis=2)
        block_mask = valid_flat[None, :] & jnp.logical_not(on_slash)
        key_place = (blocks_flat[:, None] * BLOCK_TOKENS + inner_offset[None, :]).reshape(-1)
        vert_mask = jnp.broadcast_to(
            block_mask[:, None, :, None], (per_dev, BLOCK_TOKENS, slot_count, BLOCK_TOKENS)
        ).reshape(tokens, slot_count * BLOCK_TOKENS)
        vert_mask = vert_mask & (key_place[None, :] <= query_place[:, None])
        group_slab = extended[:, :, :, kv_index, :]
        ext_index = local_index[:, None] + per_dev - offsets[None, :]
        slash_rows = group_slab[:, ext_index]
        diagonal_scores = (
            jnp.einsum(
                "hax,hisx->hais",
                query_head.reshape(per_dev, BLOCK_TOKENS, HEAD_SIZE),
                slash_rows[0],
                preferred_element_type=jnp.float32,
            )
            * scale_of_scores
        )
        slash_valid = query_block[:, None] - offsets[None, :] >= 0
        slash_mask = slash_valid[:, None, :, None] & (
            (offsets[None, None, :, None] > 0)
            | (inner_offset[None, None, None, :] <= inner_offset[None, :, None, None])
        )
        slash_mask = slash_mask.reshape(tokens, NS * BLOCK_TOKENS)
        per_head.append(
            attend(
                vert_scores,
                vert_mask,
                diagonal_scores.reshape(tokens, NS * BLOCK_TOKENS),
                slash_mask,
                vert_values,
                slash_rows[1],
                per_dev,
            )
        )
    attended = jnp.concatenate(per_head, axis=1)
    projected = jnp.dot(
        lax.all_gather(attended, "head", axis=1, tiled=True),
        out_weight,
        preferred_element_type=jnp.float32,
    )
    return projected.astype(jnp.bfloat16)


def solution(mesh):
    in_specs = (
        P("ctx", "head"),
        P("ctx", "head"),
        P("ctx", "head"),
        P("head", None),
        P("head", None, None),
        P("head", None, None),
        P("head", None),
        P(None, "head"),
    )
    out_specs = P("ctx", "head")
    return jax.shard_map(shards, mesh=mesh, in_specs=in_specs, out_specs=out_specs, check_vma=False)
```

profile of v0, /device:TPU:0, one launch (start us, length us, event | category | flops | bytes accessed | tf_op | source)
XLA Modules:
  0.0 212.7 jit_solution(3294481750343524696)
XLA Ops:
  6.5 1.1 pad_maximum_fusion.1
  7.7 5.7 %collective-permute-start = (bf16[2,512,256]{2,1,0:T(8,128)(2,1)S(1)}, bf16[2,512,256]{2,1,0:T(8,128)(2,1)}, u32[]{:S(2)}, u32[]{:S(2)}) collective-permute-start(bf16[2,512,256]{2,1,0:T(8,128)(2,1)S(1)} %pad_maximum_fusion.1), channel_id=1, source_target_pairs={{0,4},{4,8},{8,12},{12,16},{16,20},{20,24},{24,28},{1,5},{5,9},{9,... | collective-permute-start | bytes 1572872 | tf_op jit(solution)/shard_map/ppermute | solution.py:16
  13.4 1.0 stack.16
  14.4 1.0 stack.15
  15.9 1.2 gather_fusion.1
  25.8 3.2 %reshape.1866 = pred[512,1024]{0,1:T(32,128)(4,1)} reshape(pred[8,64,16,64]{1,0,3,2:T(8,128)(4,1)S(1)} %broadcast_in_dim.42) | data formatting | bytes 1048576 | tf_op jit(solution)/shard_map/reshape | solution.py:99
  30.1 2.7 %reshape.1870 = pred[512,1024]{0,1:T(32,128)(4,1)} reshape(pred[8,64,16,64]{1,0,3,2:T(8,128)(4,1)S(1)} %broadcast_in_dim.47) | data formatting | bytes 1048576 | tf_op jit(solution)/shard_map/reshape | solution.py:99
  33.9 2.7 %reshape.1873 = pred[512,1024]{0,1:T(32,128)(4,1)} reshape(pred[8,64,16,64]{1,0,3,2:T(8,128)(4,1)S(1)} %broadcast_in_dim.48) | data formatting | bytes 1048576 | tf_op jit(solution)/shard_map/reshape | solution.py:99
  37.8 2.7 %reshape.1876 = pred[512,1024]{0,1:T(32,128)(4,1)} reshape(pred[8,64,16,64]{1,0,3,2:T(8,128)(4,1)S(1)} %broadcast_in_dim.49) | data formatting | bytes 1048576 | tf_op jit(solution)/shard_map/reshape | solution.py:99
  41.6 2.7 %reshape.1879 = pred[512,1024]{0,1:T(32,128)(4,1)} reshape(pred[8,64,16,64]{1,0,3,2:T(8,128)(4,1)S(1)} %broadcast_in_dim.50) | data formatting | bytes 1048576 | tf_op jit(solution)/shard_map/reshape | solution.py:99
  45.4 2.7 %reshape.1882 = pred[512,1024]{0,1:T(32,128)(4,1)} reshape(pred[8,64,16,64]{1,0,3,2:T(8,128)(4,1)S(1)} %broadcast_in_dim.51) | data formatting | bytes 1048576 | tf_op jit(solution)/shard_map/reshape | solution.py:99
  49.2 2.7 %reshape.1885 = pred[512,1024]{0,1:T(32,128)(4,1)} reshape(pred[8,64,16,64]{1,0,3,2:T(8,128)(4,1)S(1)} %broadcast_in_dim.52) | data formatting | bytes 1048576 | tf_op jit(solution)/shard_map/reshape | solution.py:99
  53.1 2.7 %reshape.1888 = pred[512,1024]{0,1:T(32,128)(4,1)} reshape(pred[8,64,16,64]{1,0,3,2:T(8,128)(4,1)S(1)} %broadcast_in_dim.53) | data formatting | bytes 1048576 | tf_op jit(solution)/shard_map/reshape | solution.py:99
  56.4 0.9 broadcast_or_fusion
  57.3 0.9 fusion.125
  58.2 1.1 maximum_maximum_fusion
  59.7 2.4 %fusion.127 = (bf16[2,16,64,1,128]{4,3,2,1,0:T(2,128)(2,1)S(1)}, bf16[2,16,64,1,128]{4,3,2,1,0:T(2,128)(2,1)S(1)}) fusion(bf16[2,16,64,2,128]{4,3,2,1,0:T(2,128)(2,1)S(1)} %reshape.1867), kind=kLoop, calls=%fused_computation.287 | loop fusion | bytes 2097152 | tf_op jit(solution)/shard_map/slice | solution.py:101
  63.7 1.0 copy-done.16
  64.6 1.3 fusion.133
  67.5 1.0 copy-done.15
  68.5 1.3 fusion.135
  71.4 1.0 copy-done.14
  72.3 1.3 fusion.137
  75.2 1.0 copy-done.13
  76.2 1.3 fusion.139
  79.1 1.0 copy-done.12
  80.1 1.4 fusion.141
  83.0 1.1 copy-done.11
  85.3 1.0 copy-done.9
  86.8 1.7 gather_fusion.9
  88.4 1.3 copy.164
  89.7 1.0 copy-done.7
  91.2 2.2 %fusion.126 = (bf16[1,16,2,64,128]{4,3,2,1,0:T(8,128)(2,1)}, bf16[1,16,2,64,128]{4,3,2,1,0:T(8,128)(2,1)S(1)}) fusion(bf16[2,16,2,64,128]{4,3,2,1,0:T(8,128)(2,1)} %all-gather.6.cloned.1.call-done), kind=kLoop, calls=%fused_computation.286 | loop fusion | bytes 2097152 | tf_op jit(solution)/shard_map/slice | solution.py:83
  93.4 0.8 fusion.129
  94.2 3.0 %fusion.132 = (f32[512]{0:T(512)S(1)}, f32[512,1024]{0,1:T(8,128)}) fusion(bf16[1024,128]{1,0:T(8,128)(2,1)S(1)} %bitcast.377, bf16[512,1024]{1,0:T(8,128)(2,1)} %param.8, pred[512,1024]{0,1:T(32,128)(4,1)S(1)} %copy-done.42, s32[512]{0:T(512)S(1)} %copy-done.102, s32[1024]{0:T(1024)S(1)} %copy-done.99), kind=kOutput, calls=%fused_computation.292 | convolution fusion | flops 136838656 | bytes 3022848 | tf_op jit(solution)/shard_map/qd,kd->qk/dot_general | solution.py:90
  97.3 1.8 fusion.102
  99.3 2.9 %fusion.134 = (f32[512]{0:T(512)S(1)}, f32[512,1024]{0,1:T(8,128)}) fusion(bf16[1024,128]{1,0:T(8,128)(2,1)S(1)} %bitcast.378, bf16[512,1024]{1,0:T(8,128)(2,1)} %param.8, pred[512,1024]{0,1:T(32,128)(4,1)S(1)} %copy-done.41, s32[512]{0:T(512)S(1)} %copy-done.102, s32[1024]{0:T(1024)S(1)} %copy-done.98), kind=kOutput, calls=%fused_computation.294 | convolution fusion | flops 136838656 | bytes 3022848 | tf_op jit(solution)/shard_map/qd,kd->qk/dot_general | solution.py:90
  102.3 2.5 %fusion.100 = f32[8,64,128,1]{2,1,3,0:T(8,128)} fusion(f32[8,64,4,64]{1,3,2,0:T(8,128)} %get-tuple-element.84, bf16[2,8,4,64,128]{4,3,2,1,0:T(8,128)(2,1)} %bitcast.347, f32[8,64]{1,0:T(8,128)S(1)} %max.91), kind=kOutput, calls=%fused_computation.138 | convolution fusion | flops 33816576 | bytes 1837056 | tf_op jit(solution)/shard_map/wojf,wjfl->wol/dot_general | solution.py:37
  105.0 2.9 %fusion.136 = (f32[512]{0:T(512)S(1)}, f32[512,1024]{0,1:T(8,128)}) fusion(bf16[1024,128]{1,0:T(8,128)(2,1)S(1)} %bitcast.379, bf16[512,1024]{1,0:T(8,128)(2,1)} %param.8, pred[512,1024]{0,1:T(32,128)(4,1)S(1)} %copy-done.40, s32[512]{0:T(512)S(1)} %copy-done.102, s32[1024]{0:T(1024)S(1)} %copy-done.97), kind=kOutput, calls=%fused_computation.296 | convolution fusion | flops 136838656 | bytes 3022848 | tf_op jit(solution)/shard_map/qd,kd->qk/dot_general | solution.py:90
  108.0 2.5 %fusion.98 = f32[8,64,128,1]{2,1,3,0:T(8,128)} fusion(f32[8,64,4,64]{1,3,2,0:T(8,128)} %get-tuple-element.88, bf16[2,8,4,64,128]{4,3,2,1,0:T(8,128)(2,1)} %bitcast.345, f32[8,64]{1,0:T(8,128)S(1)} %max.93), kind=kOutput, calls=%fused_computation.137 | convolution fusion | flops 33816576 | bytes 1837056 | tf_op jit(solution)/shard_map/wojf,wjfl->wol/dot_general | solution.py:37
  110.8 2.9 %fusion.138 = (f32[512]{0:T(512)S(1)}, f32[512,1024]{0,1:T(8,128)}) fusion(bf16[1024,128]{1,0:T(8,128)(2,1)S(1)} %bitcast.380, bf16[512,1024]{1,0:T(8,128)(2,1)} %param.8, pred[512,1024]{0,1:T(32,128)(4,1)S(1)} %copy-done.39, s32[512]{0:T(512)S(1)} %copy-done.102, s32[1024]{0:T(1024)S(1)} %copy-done.96), kind=kOutput, calls=%fused_computation.298 | convolution fusion | flops 136838656 | bytes 3022848 | tf_op jit(solution)/shard_map/qd,kd->qk/dot_general | solution.py:90
  113.8 2.5 %fusion.96 = f32[8,64,128,1]{2,1,3,0:T(8,128)} fusion(f32[8,64,4,64]{1,3,2,0:T(8,128)} %get-tuple-element.92, bf16[2,8,4,64,128]{4,3,2,1,0:T(8,128)(2,1)} %bitcast.343, f32[8,64]{1,0:T(8,128)S(1)} %max.95), kind=kOutput, calls=%fused_computation.136 | convolution fusion | flops 33816576 | bytes 1837056 | tf_op jit(solution)/shard_map/wojf,wjfl->wol/dot_general | solution.py:37
  117.4 3.0 %fusion.140 = (f32[512]{0:T(512)S(1)}, f32[512,1024]{0,1:T(8,128)}) fusion(bf16[1024,128]{1,0:T(8,128)(2,1)S(1)} %bitcast.373, bf16[512,1024]{1,0:T(8,128)(2,1)} %param.8, pred[512,1024]{0,1:T(32,128)(4,1)S(1)} %copy-done.38, s32[512]{0:T(512)S(1)} %copy-done.102, s32[1024]{0:T(1024)S(1)} %copy-done.95), kind=kOutput, calls=%fused_computation.300 | convolution fusion | flops 136838656 | bytes 3022848 | tf_op jit(solution)/shard_map/qd,kd->qk/dot_general | solution.py:90
  120.5 2.5 %fusion.94 = f32[8,64,128,1]{2,1,3,0:T(8,128)} fusion(f32[8,64,4,64]{1,3,2,0:T(8,128)} %get-tuple-element.96, bf16[2,8,4,64,128]{4,3,2,1,0:T(8,128)(2,1)} %bitcast.341, f32[8,64]{1,0:T(8,128)S(1)} %max.97), kind=kOutput, calls=%fused_computation.135 | convolution fusion | flops 33816576 | bytes 1837056 | tf_op jit(solution)/shard_map/wojf,wjfl->wol/dot_general | solution.py:37
  123.2 3.1 %fusion.142 = (f32[512]{0:T(512)S(1)}, f32[512,1024]{0,1:T(8,128)}) fusion(bf16[1024,128]{1,0:T(8,128)(2,1)S(1)} %bitcast.374, bf16[512,1024]{1,0:T(8,128)(2,1)} %param.8, pred[512,1024]{0,1:T(32,128)(4,1)S(1)} %copy-done.37, s32[512]{0:T(512)S(1)} %copy-done.102, s32[1024]{0:T(1024)S(1)} %copy-done.94), kind=kOutput, calls=%fused_computation.302 | convolution fusion | flops 136838656 | bytes 3022848 | tf_op jit(solution)/shard_map/qd,kd->qk/dot_general | solution.py:90
  126.4 2.2 %fusion.92 = f32[8,64,128,1]{2,1,3,0:T(8,128)} fusion(f32[8,64,4,64]{1,3,2,0:T(8,128)S(1)} %get-tuple-element.100, bf16[2,8,4,64,128]{4,3,2,1,0:T(8,128)(2,1)} %bitcast.339, f32[8,64]{1,0:T(8,128)S(1)} %max.99), kind=kOutput, calls=%fused_computation.134 | convolution fusion | flops 33816576 | bytes 1312768 | tf_op jit(solution)/shard_map/wojf,wjfl->wol/dot_general | solution.py:37
  128.8 3.0 %fusion.144 = (f32[512]{0:T(512)S(1)}, f32[512,1024]{0,1:T(8,128)}) fusion(bf16[1024,128]{1,0:T(8,128)(2,1)S(1)} %bitcast.375, bf16[512,1024]{1,0:T(8,128)(2,1)} %param.8, pred[512,1024]{0,1:T(32,128)(4,1)S(1)} %copy-done.36, s32[512]{0:T(512)S(1)} %copy-done.102, s32[1024]{0:T(1024)S(1)} %copy-done.93), kind=kOutput, calls=%fused_computation.304 | convolution fusion | flops 136838656 | bytes 3022848 | tf_op jit(solution)/shard_map/qd,kd->qk/dot_general | solution.py:90
  131.9 1.0 fusion.90
  133.1 3.0 %fusion.146 = (f32[512]{0:T(512)S(1)}, f32[512,1024]{0,1:T(8,128)}) fusion(bf16[1024,128]{1,0:T(8,128)(2,1)S(1)} %bitcast.376, bf16[512,1024]{1,0:T(8,128)(2,1)} %param.8, pred[512,1024]{0,1:T(32,128)(4,1)S(1)} %copy-done.35, s32[512]{0:T(512)S(1)} %copy-done.102, s32[1024]{0:T(1024)S(1)} %copy-done.92), kind=kOutput, calls=%fused_computation.306 | convolution fusion | flops 136838656 | bytes 3022848 | tf_op jit(solution)/shard_map/qd,kd->qk/dot_general | solution.py:90
  136.2 1.0 fusion.88
  137.4 0.8 copy.130
  138.4 1.9 copy.135
  140.3 1.8 copy.140
  142.2 0.8 copy.145
  143.1 0.8 copy.151
  144.0 0.8 copy.156
  144.9 0.8 copy.161
  145.9 0.9 copy.166
  147.2 1.2 copy-done.20
  151.1 0.8 copy-done.24
  152.8 0.8 copy-done.26
  160.4 1.0 copy-done.34
  161.3 34.1 %all-gather.4.cloned.1.call-done = bf16[512,4096]{0,1:T(8,128)(2,1)} async-done(((bf16[512,1024]{0,1:T(8,128)(2,1)}), bf16[512,4096]{0,1:T(8,128)(2,1)}) %all-gather.4.cloned.1.call-update) | async-done | bytes 4194320 | tf_op jit(solution)/shard_map/all_gather | solution.py:132
  195.5 10.1 %convolution_convert_fusion = bf16[512,1024]{1,0:T(8,128)(2,1)} fusion(bf16[512,4096]{0,1:T(8,128)(2,1)} %all-gather.4.cloned.1.call-done, bf16[4096,1024]{1,0:T(8,128)(2,1)} %param.15), kind=kOutput, calls=%fused_computation.42 | convolution fusion | flops 4295491584 | bytes 13631488 | tf_op jit(solution)/shard_map/dot_general | solution.py:131
  (425 shorter events, 43.1 us)
Async XLA Ops:
  6.5 9.0 %copy-start = (s32[2,8,2]{1,2,0:T(2,128)S(1)}, s32[2,8,2]{1,2,0:T(2,128)}, u32[]{:S(2)}) copy-start(s32[2,8,2]{1,2,0:T(2,128)} %param.12) | copy-start | bytes 388
  6.5 84.6 %all-gather.6.cloned.1.call-start = ((), (), s32[]{:S(2)}) async-start(), calls=%async_computation.1 | async-start | bytes 1179648 | tf_op jit(solution)/shard_map/all_gather | solution.py:69
  6.5 10.7 %copy-start.66 = (s32[8,4]{0,1:T(4,128)S(1)}, s32[8,4]{0,1:T(4,128)}, u32[]{:S(2)}) copy-start(s32[8,4]{0,1:T(4,128)} %param.11) | copy-start | bytes 388
  7.6 13.0 %copy-start.100 = (s32[8,8]{1,0:T(8,128)S(1)}, s32[8,8]{1,0:T(8,128)}, u32[]{:S(2)}) copy-start(s32[8,8]{1,0:T(8,128)} %param.14) | copy-start | bytes 772
  7.7 13.0 %copy-start.101 = (s32[8,8,1]{1,2,0:T(1,128)S(1)}, s32[8,8,1]{1,2,0:T(1,128)}, u32[]{:S(2)}) copy-start(s32[8,8,1]{1,2,0:T(1,128)} %param.13) | copy-start | bytes 772
  7.7 50.6 %collective-permute-start = (bf16[2,512,256]{2,1,0:T(8,128)(2,1)S(1)}, bf16[2,512,256]{2,1,0:T(8,128)(2,1)}, u32[]{:S(2)}, u32[]{:S(2)}) collective-permute-start(bf16[2,512,256]{2,1,0:T(8,128)(2,1)S(1)} %pad_maximum_fusion.1), channel_id=1, source_target_pairs={{0,4},{4,8},{8,12},{12,16},{16,20},{20,24},{24,28},{1,5},{5,9},{9,... | collective-permute-start | bytes 1572872 | tf_op jit(solution)/shard_map/ppermute | solution.py:16
  17.1 178.4 %all-gather.4.cloned.1.call-start = ((), (), s32[]{:S(2)}) async-start(), calls=%async_computation | async-start | bytes 5242880 | tf_op jit(solution)/shard_map/all_gather | solution.py:132
  49.2 8.1 %copy-start.33 = (bf16[512,1024]{1,0:T(8,128)(2,1)S(1)}, bf16[512,1024]{1,0:T(8,128)(2,1)}, u32[]{:S(2)}) copy-start(bf16[512,1024]{1,0:T(8,128)(2,1)} %param.8) | copy-start | bytes 3145732
  53.0 5.2 %copy-start.17 = (bf16[512,256]{1,0:T(8,128)(2,1)S(1)}, bf16[512,256]{1,0:T(8,128)(2,1)}, u32[]{:S(2)}) copy-start(bf16[512,256]{1,0:T(8,128)(2,1)} %param.10) | copy-start | bytes 786436
  53.0 5.2 %copy-start.18 = (bf16[512,256]{1,0:T(8,128)(2,1)S(1)}, bf16[512,256]{1,0:T(8,128)(2,1)}, u32[]{:S(2)}) copy-start(bf16[512,256]{1,0:T(8,128)(2,1)} %param.9) | copy-start | bytes 786436
  63.5 3.1 %copy-start.75 = (s32[1024]{0:T(1024)S(1)}, s32[1024]{0:T(1024)}, u32[]{:S(2)}) copy-start(s32[1024]{0:T(1024)} %get-tuple-element.115) | copy-start | bytes 12292
  67.4 3.1 %copy-start.77 = (s32[1024]{0:T(1024)S(1)}, s32[1024]{0:T(1024)}, u32[]{:S(2)}) copy-start(s32[1024]{0:T(1024)} %get-tuple-element.114) | copy-start | bytes 12292
  74.3 1.9 copy-start.62
  74.3 1.9 copy-start.71
  74.3 1.9 copy-start.107
  75.1 3.1 %copy-start.76 = (s32[1024]{0:T(1024)S(1)}, s32[1024]{0:T(1024)}, u32[]{:S(2)}) copy-start(s32[1024]{0:T(1024)} %get-tuple-element.112) | copy-start | bytes 12292
  86.7 4.0 %copy-start.67 = (pred[64,4,64]{0,2,1:T(8,128)(4,1)S(1)}, pred[64,4,64]{0,2,1:T(8,128)(4,1)}, u32[]{:S(2)}) copy-start(pred[64,4,64]{0,2,1:T(8,128)(4,1)} %get-tuple-element.45) | copy-start | bytes 49156
  86.8 4.0 %copy-start.103 = (pred[8,4]{1,0:T(8,128)(4,1)S(1)}, pred[8,4]{1,0:T(8,128)(4,1)}, u32[]{:S(2)}) copy-start(pred[8,4]{1,0:T(8,128)(4,1)} %get-tuple-element.61) | copy-start | bytes 100
  91.2 3.0 %copy-start.99 = (s32[1024]{0:T(1024)S(1)}, s32[1024]{0:T(1024)}, u32[]{:S(2)}) copy-start(s32[1024]{0:T(1024)} %add.426) | copy-start | bytes 12292
  91.2 3.0 %copy-start.102 = (s32[512]{0:T(512)S(1)}, s32[512]{0:T(512)}, u32[]{:S(2)}) copy-start(s32[512]{0:T(512)} %iota_add_fusion.8) | copy-start | bytes 6148
  91.2 3.0 %copy-start.42 = (pred[512,1024]{0,1:T(32,128)(4,1)S(1)}, pred[512,1024]{0,1:T(32,128)(4,1)}, u32[]{:S(2)}) copy-start(pred[512,1024]{0,1:T(32,128)(4,1)} %reshape.1866) | copy-start | bytes 1572868
  93.4 3.9 %copy-start.86 = (f32[8,64]{1,0:T(8,128)S(1)}, f32[8,64]{1,0:T(8,128)}, u32[]{:S(2)}) copy-start(f32[8,64]{1,0:T(8,128)} %copy-done.85) | copy-start | bytes 6148
  94.1 3.0 %copy-start.57 = (bf16[8,2,1,64,128]{4,3,1,0,2:T(8,128)(2,1)}, bf16[8,2,1,64,128]{4,3,1,0,2:T(8,128)(2,1)S(1)}, u32[]{:S(2)}) copy-start(bf16[8,2,1,64,128]{4,3,1,0,2:T(8,128)(2,1)S(1)} %get-tuple-element.28) | copy-start | bytes 786436
  97.2 2.1 copy-start.98
  97.2 2.1 copy-start.41
  97.3 2.1 copy-start.58
  99.1 3.2 %copy-start.84 = (f32[8,64]{1,0:T(8,128)S(1)}, f32[8,64]{1,0:T(8,128)}, u32[]{:S(2)}) copy-start(f32[8,64]{1,0:T(8,128)} %copy-done.83) | copy-start | bytes 6148
  102.2 2.8 %copy-start.97 = (s32[1024]{0:T(1024)S(1)}, s32[1024]{0:T(1024)}, u32[]{:S(2)}) copy-start(s32[1024]{0:T(1024)} %add.445) | copy-start | bytes 12292
  102.3 2.5 %copy-start.5 = (f32[8,64,4,64]{1,3,2,0:T(8,128)S(1)}, f32[8,64,4,64]{1,3,2,0:T(8,128)}, u32[]{:S(2)}) copy-start(f32[8,64,4,64]{1,3,2,0:T(8,128)} %get-tuple-element.84) | copy-start | bytes 1572868
  102.3 2.7 %copy-start.40 = (pred[512,1024]{0,1:T(32,128)(4,1)S(1)}, pred[512,1024]{0,1:T(32,128)(4,1)}, u32[]{:S(2)}) copy-start(pred[512,1024]{0,1:T(32,128)(4,1)} %reshape.1873) | copy-start | bytes 1572868
  102.3 2.7 %copy-start.59 = (bf16[8,2,1,64,128]{4,3,1,0,2:T(8,128)(2,1)S(1)}, bf16[8,2,1,64,128]{4,3,1,0,2:T(8,128)(2,1)}, u32[]{:S(2)}) copy-start(bf16[8,2,1,64,128]{4,3,1,0,2:T(8,128)(2,1)} %copy-done.57) | copy-start | bytes 786436
  104.8 3.2 %copy-start.82 = (f32[8,64]{1,0:T(8,128)S(1)}, f32[8,64]{1,0:T(8,128)}, u32[]{:S(2)}) copy-start(f32[8,64]{1,0:T(8,128)} %copy-done.81) | copy-start | bytes 6148
  107.9 2.8 %copy-start.96 = (s32[1024]{0:T(1024)S(1)}, s32[1024]{0:T(1024)}, u32[]{:S(2)}) copy-start(s32[1024]{0:T(1024)} %add.452) | copy-start | bytes 12292
  108.0 2.5 %copy-start.4 = (f32[8,64,4,64]{1,3,2,0:T(8,128)S(1)}, f32[8,64,4,64]{1,3,2,0:T(8,128)}, u32[]{:S(2)}) copy-start(f32[8,64,4,64]{1,3,2,0:T(8,128)} %get-tuple-element.88) | copy-start | bytes 1572868
  108.0 2.7 %copy-start.39 = (pred[512,1024]{0,1:T(32,128)(4,1)S(1)}, pred[512,1024]{0,1:T(32,128)(4,1)}, u32[]{:S(2)}) copy-start(pred[512,1024]{0,1:T(32,128)(4,1)} %reshape.1876) | copy-start | bytes 1572868
  108.0 2.8 %copy-start.60 = (bf16[8,2,1,64,128]{4,3,1,0,2:T(8,128)(2,1)S(1)}, bf16[8,2,1,64,128]{4,3,1,0,2:T(8,128)(2,1)}, u32[]{:S(2)}) copy-start(bf16[8,2,1,64,128]{4,3,1,0,2:T(8,128)(2,1)} %copy-done.57) | copy-start | bytes 786436
  110.6 3.2 %copy-start.80 = (f32[8,64]{1,0:T(8,128)S(1)}, f32[8,64]{1,0:T(8,128)}, u32[]{:S(2)}) copy-start(f32[8,64]{1,0:T(8,128)} %copy-done.79) | copy-start | bytes 6148
  113.8 2.6 %copy-start.3 = (f32[8,64,4,64]{1,3,2,0:T(8,128)S(1)}, f32[8,64,4,64]{1,3,2,0:T(8,128)}, u32[]{:S(2)}) copy-start(f32[8,64,4,64]{1,3,2,0:T(8,128)} %get-tuple-element.92) | copy-start | bytes 1572868
  113.8 2.8 %copy-start.27 = (bf16[1,16,2,64,128]{4,3,2,1,0:T(8,128)(2,1)S(1)}, bf16[1,16,2,64,128]{4,3,2,1,0:T(8,128)(2,1)}, u32[]{:S(2)}) copy-start(bf16[1,16,2,64,128]{4,3,2,1,0:T(8,128)(2,1)} %get-tuple-element.21) | copy-start | bytes 1572868
  113.8 3.6 %copy-start.38 = (pred[512,1024]{0,1:T(32,128)(4,1)S(1)}, pred[512,1024]{0,1:T(32,128)(4,1)}, u32[]{:S(2)}) copy-start(pred[512,1024]{0,1:T(32,128)(4,1)} %reshape.1879) | copy-start | bytes 1572868
  113.8 3.6 %copy-start.95 = (s32[1024]{0:T(1024)S(1)}, s32[1024]{0:T(1024)}, u32[]{:S(2)}) copy-start(s32[1024]{0:T(1024)} %add.459) | copy-start | bytes 12292
  117.3 3.0 %copy-start.53 = (bf16[8,2,1,64,128]{4,3,1,0,2:T(8,128)(2,1)}, bf16[8,2,1,64,128]{4,3,1,0,2:T(8,128)(2,1)S(1)}, u32[]{:S(2)}) copy-start(bf16[8,2,1,64,128]{4,3,1,0,2:T(8,128)(2,1)S(1)} %get-tuple-element.26) | copy-start | bytes 786436
  120.4 2.8 %copy-start.94 = (s32[1024]{0:T(1024)S(1)}, s32[1024]{0:T(1024)}, u32[]{:S(2)}) copy-start(s32[1024]{0:T(1024)} %add.466) | copy-start | bytes 12292
  120.5 2.5 %copy-start.2 = (f32[8,64,4,64]{1,3,2,0:T(8,128)S(1)}, f32[8,64,4,64]{1,3,2,0:T(8,128)}, u32[]{:S(2)}) copy-start(f32[8,64,4,64]{1,3,2,0:T(8,128)} %get-tuple-element.96) | copy-start | bytes 1572868
  120.5 2.7 %copy-start.37 = (pred[512,1024]{0,1:T(32,128)(4,1)S(1)}, pred[512,1024]{0,1:T(32,128)(4,1)}, u32[]{:S(2)}) copy-start(pred[512,1024]{0,1:T(32,128)(4,1)} %reshape.1882) | copy-start | bytes 1572868
  120.5 2.7 %copy-start.54 = (bf16[8,2,1,64,128]{4,3,1,0,2:T(8,128)(2,1)S(1)}, bf16[8,2,1,64,128]{4,3,1,0,2:T(8,128)(2,1)}, u32[]{:S(2)}) copy-start(bf16[8,2,1,64,128]{4,3,1,0,2:T(8,128)(2,1)} %copy-done.53) | copy-start | bytes 786436
  126.3 2.4 %copy-start.93 = (s32[1024]{0:T(1024)S(1)}, s32[1024]{0:T(1024)}, u32[]{:S(2)}) copy-start(s32[1024]{0:T(1024)} %add.473) | copy-start | bytes 12292
  126.4 2.4 %copy-start.36 = (pred[512,1024]{0,1:T(32,128)(4,1)S(1)}, pred[512,1024]{0,1:T(32,128)(4,1)}, u32[]{:S(2)}) copy-start(pred[512,1024]{0,1:T(32,128)(4,1)} %reshape.1885) | copy-start | bytes 1572868
  126.4 2.4 %copy-start.55 = (bf16[8,2,1,64,128]{4,3,1,0,2:T(8,128)(2,1)S(1)}, bf16[8,2,1,64,128]{4,3,1,0,2:T(8,128)(2,1)}, u32[]{:S(2)}) copy-start(bf16[8,2,1,64,128]{4,3,1,0,2:T(8,128)(2,1)} %copy-done.53) | copy-start | bytes 786436
  128.8 3.1 %copy-start.10 = (bf16[32,2,64,128]{3,2,0,1:T(8,128)(2,1)S(1)}, bf16[32,2,64,128]{3,2,0,1:T(8,128)(2,1)}, u32[]{:S(2)}) copy-start(bf16[32,2,64,128]{3,2,0,1:T(8,128)(2,1)} %copy-done.9) | copy-start | bytes 3145732
  132.9 3.3 %copy-start.8 = (bf16[32,2,64,128]{3,2,0,1:T(8,128)(2,1)S(1)}, bf16[32,2,64,128]{3,2,0,1:T(8,128)(2,1)}, u32[]{:S(2)}) copy-start(bf16[32,2,64,128]{3,2,0,1:T(8,128)(2,1)} %copy-done.7) | copy-start | bytes 3145732
  136.1 2.2 %copy-start.87 = (f32[512]{0:T(512)S(1)}, f32[512]{0:T(512)}, u32[]{:S(2)}) copy-start(f32[512]{0:T(512)} %reduce_max.178) | copy-start | bytes 6148
  136.1 4.2 %copy-start.88 = (f32[512]{0:T(512)S(1)}, f32[512]{0:T(512)}, u32[]{:S(2)}) copy-start(f32[512]{0:T(512)} %reduce_max.182) | copy-start | bytes 6148
  136.2 5.9 %copy-start.89 = (f32[512]{0:T(512)S(1)}, f32[512]{0:T(512)}, u32[]{:S(2)}) copy-start(f32[512]{0:T(512)} %reduce_max.186) | copy-start | bytes 6148
  136.2 6.9 %copy-start.90 = (f32[512]{0:T(512)S(1)}, f32[512]{0:T(512)}, u32[]{:S(2)}) copy-start(f32[512]{0:T(512)} %reduce_max.190) | copy-start | bytes 6148
  137.2 5.0 %copy-start.28 = (f32[8,64,128,1]{2,1,3,0:T(8,128)S(1)}, f32[8,64,128,1]{2,1,3,0:T(8,128)}, u32[]{:S(2)}) copy-start(f32[8,64,128,1]{2,1,3,0:T(8,128)} %fusion.96) | copy-start | bytes 786436
  137.2 5.9 %copy-start.29 = (f32[8,64,128,1]{2,1,3,0:T(8,128)S(1)}, f32[8,64,128,1]{2,1,3,0:T(8,128)}, u32[]{:S(2)}) copy-start(f32[8,64,128,1]{2,1,3,0:T(8,128)} %fusion.94) | copy-start | bytes 786436
  137.2 6.7 %copy-start.91 = (f32[512]{0:T(512)S(1)}, f32[512]{0:T(512)}, u32[]{:S(2)}) copy-start(f32[512]{0:T(512)} %reduce_max.194) | copy-start | bytes 6148
  137.2 6.8 %copy-start.30 = (f32[8,64,128,1]{2,1,3,0:T(8,128)S(1)}, f32[8,64,128,1]{2,1,3,0:T(8,128)}, u32[]{:S(2)}) copy-start(f32[8,64,128,1]{2,1,3,0:T(8,128)} %fusion.92) | copy-start | bytes 786436
  137.2 7.7 %copy-start.31 = (f32[8,64,128,1]{2,1,3,0:T(8,128)S(1)}, f32[8,64,128,1]{2,1,3,0:T(8,128)}, u32[]{:S(2)}) copy-start(f32[8,64,128,1]{2,1,3,0:T(8,128)} %fusion.90) | copy-start | bytes 786436
  137.4 9.4 %copy-start.19 = (f32[512,1024]{0,1:T(8,128)S(1)}, f32[512,1024]{0,1:T(8,128)}, u32[]{:S(2)}) copy-start(f32[512,1024]{0,1:T(8,128)} %get-tuple-element.78) | copy-start | bytes 6291460
  138.3 7.6 %copy-start.32 = (f32[8,64,128,1]{2,1,3,0:T(8,128)S(1)}, f32[8,64,128,1]{2,1,3,0:T(8,128)}, u32[]{:S(2)}) copy-start(f32[8,64,128,1]{2,1,3,0:T(8,128)} %fusion.88) | copy-start | bytes 786436
  146.8 2.2 %copy-start.21 = (f32[512,1024]{0,1:T(8,128)S(1)}, f32[512,1024]{0,1:T(8,128)}, u32[]{:S(2)}) copy-start(f32[512,1024]{0,1:T(8,128)} %get-tuple-element.86) | copy-start | bytes 6291460
  195.5 10.1 %copy-start.1 = (s32[2,8,2]{1,2,0:T(2,128)S(1)}, s32[2,8,2]{1,2,0:T(2,128)}, u32[]{:S(2)}) copy-start(s32[2,8,2]{1,2,0:T(2,128)} %param.12) | copy-start | bytes 388
  (50 other events, 72.0 us)
Sparse Core Ops, SparseCore 0:
  17.3 39.9 all-gather.5
  161.5 33.9 all-gather.3
where the time goes:
time: 216 us; the launch traced here: 213 us
  local copies, waits for them, and re-layouts  84.3 us (39%)
  matrix products  61.5 us (28%)
  waiting for transfers between devices  34.2 us (16%)
  between operations  14.9 us (7%)
  other arithmetic  12.1 us (6%)
  starting transfers between devices  5.73 us (3%)
    all_gather x1, waiting for transfers between devices, shards(): lax.all_gather(attended, 'head', axis=1, tiled=True)  34.1 us
    dot_general x8, matrix products, shards(): jnp.einsum('qd,kd->qk', query_head, vert_keys, preferred_element_type=jnp...  23.8 us
    reshape x8, local copies, waits for them, and re-layouts, shards(): vert_mask = jnp.broadcast_to(block_mask[:, None, :, None], (per_dev, BLOC...  22.2 us
    unnamed x223, local copies, waits for them, and re-layouts  16.7 us
    dot_general x8, matrix products, attend(): jnp.einsum('wojf,wjfl->wol', slash_probability, diagonal_values, preferre...  16.1 us
    dot_general x1, matrix products, shards(): jnp.dot(lax.all_gather(attended, 'head', axis=1, tiled=True), out_weight,...  10.1 us
    gather x16, local copies, waits for them, and re-layouts, shards(): slash_rows = group_slab[:, ext_index]  8.74 us
    reshape x8, local copies, waits for them, and re-layouts, attend(): numer = numer + diagonal_portion.reshape(per_dev * BLOCK_TOKENS, HEAD_SIZE)  8.7 us
  transfers between devices with their start and end apart: 3, of which 1 were waited for; matrix products, arithmetic and copies ran while one was open for 32% of the time, Pallas kernels for 0%

commit v1 on v0

v1 whole, which is shorter than its diff:
```python
import functools

import jax
import jax.numpy as jnp
from jax import lax
from jax.experimental import pallas as pl
from jax.experimental.pallas import tpu as pltpu
from jax.sharding import PartitionSpec as P


HEAD_SIZE = 128
BLOCK = 64
PAIR = 2 * BLOCK
LOG2E = 1.4426950408889634
SCALE2 = HEAD_SIZE**-0.5 * LOG2E
HIDE = -1e30
CONTRACT = (((1,), (1,)), ((), ()))


def prep_body(unions, keys, values, *outs, groups, union):
    rank = lax.axis_index("ctx")
    blocks = outs[groups]
    for g in range(groups):
        cols = pl.ds(g * HEAD_SIZE, HEAD_SIZE)
        outs[g][:, :HEAD_SIZE] = keys[:, cols]
        outs[g][:, HEAD_SIZE:] = values[:, cols]
        for u in range(union):
            start = pl.multiple_of(unions[g, rank, u] * BLOCK, BLOCK)
            rows = pl.ds((g * union + u) * BLOCK, BLOCK)
            blocks[rows, :HEAD_SIZE] = keys[pl.ds(start, BLOCK), cols]
            blocks[rows, HEAD_SIZE:] = values[pl.ds(start, BLOCK), cols]


def smem():
    return pl.BlockSpec(memory_space=pltpu.SMEM)


def vmem():
    return pl.BlockSpec(memory_space=pltpu.VMEM)


def prep(unions, keys, values, groups, union):
    tokens = keys.shape[0]
    wide = 2 * HEAD_SIZE
    return pl.pallas_call(
        functools.partial(prep_body, groups=groups, union=union),
        out_shape=[jax.ShapeDtypeStruct((tokens, wide), keys.dtype)] * groups
        + [jax.ShapeDtypeStruct((groups * union * BLOCK, wide), keys.dtype)],
        grid=(1,),
        in_specs=[smem()] + [pl.BlockSpec(keys.shape, lambda p: (0, 0))] * 2,
        out_specs=[vmem()] * (groups + 1),
        compiler_params=pltpu.CompilerParams(vmem_limit_bytes=8 << 20),
        name="prep",
    )(unions, keys, values)


def picked(picks, counts, head, owner, j):
    return picks[head, owner, j], j < counts[head, owner]


def near_body(
    offsets_ref, unions, picks, counts, q_ref, prev_ref, local_ref, sum_ref, peak_ref, total_ref, window,
    *, group, heads, per_dev,
):
    rank = lax.axis_index("ctx")
    tokens = per_dev * BLOCK
    wide = (per_dev + 2) * BLOCK
    window[:tokens, :] = prev_ref[...]
    window[tokens:, :] = local_ref[...]
    place = lax.broadcasted_iota(jnp.int32, (1, wide), 1) // BLOCK
    row = lax.broadcasted_iota(jnp.int32, (PAIR, PAIR), 0)
    col = lax.broadcasted_iota(jnp.int32, (PAIR, PAIR), 1)
    causal = jnp.where(row >= col, 0.0, HIDE)

    def scores_of(step):
        rows = slice(step * PAIR, (step + 1) * PAIR)
        queries = [q_ref[rows, i * HEAD_SIZE : (i + 1) * HEAD_SIZE] for i in range(heads)]
        return lax.dot_general(
            jnp.concatenate(queries, axis=0), window[step * PAIR : step * PAIR + wide, :HEAD_SIZE], CONTRACT,
            preferred_element_type=jnp.float32,
        )

    slashes, columns = [], []
    for i in range(heads):
        head = group * heads + i
        slashes.append([offsets_ref[head, s] for s in range(offsets_ref.shape[1])])
        at = []
        for j in range(picks.shape[2]):
            entry, used = picked(picks, counts, head, rank, j)
            at.append(jnp.where(used, unions[group, rank, entry] + per_dev, -tokens))
        columns.append(at)
    seen_slash = []
    for i in range(heads):
        for half in range(2):
            distance = half + per_dev - place
            seen = distance == slashes[i][0]
            for offset in slashes[i][1:]:
                seen = seen | (distance == offset)
            seen_slash.append((distance, jnp.where(seen, 0.0, HIDE)))

    steps = tokens // PAIR
    ahead = scores_of(0)
    for step in range(steps):
        near = ahead
        if step + 1 < steps:
            ahead = scores_of(step + 1)
        exists = place + (rank * per_dev - per_dev + 2 * step) >= 0
        parts = []
        for i in range(heads):
            for half in range(2):
                distance, bias = seen_slash[2 * i + half]
                for column in columns[i]:
                    bias = jnp.where((place == column - 2 * step) & (distance > 0), 0.0, bias)
                begin = i * PAIR + half * BLOCK
                piece = near[begin : begin + BLOCK] + jnp.where(exists, bias, HIDE)
                triangle = causal[half * BLOCK : (half + 1) * BLOCK]
                parts.append(
                    jnp.concatenate([piece[:, : wide - PAIR], piece[:, wide - PAIR :] + triangle], axis=1)
                )
        near = jnp.concatenate(parts, axis=0)
        peak = jnp.max(near, axis=1, keepdims=True)
        weight = jnp.exp2((near - peak) * SCALE2)
        total = jnp.sum(weight, axis=1, keepdims=True)
        sums = jnp.dot(
            weight.astype(jnp.bfloat16), window[step * PAIR : step * PAIR + wide, HEAD_SIZE:],
            preferred_element_type=jnp.float32,
        )
        out = slice(step * PAIR, (step + 1) * PAIR)
        for i in range(heads):
            rows = slice(i * PAIR, (i + 1) * PAIR)
            cols = slice(i * HEAD_SIZE, (i + 1) * HEAD_SIZE)
            sum_ref[out, cols] = sums[rows]
            peak_ref[out, cols] = jnp.broadcast_to(peak[rows], (PAIR, HEAD_SIZE))
            total_ref[out, cols] = jnp.broadcast_to(total[rows], (PAIR, HEAD_SIZE))


def attend_near(scalars, queries, prev, local, group, heads):
    tokens = queries.shape[0]
    cols = heads * HEAD_SIZE
    return pl.pallas_call(
        functools.partial(near_body, group=group, heads=heads, per_dev=tokens // BLOCK),
        grid=(1,),
        out_shape=[jax.ShapeDtypeStruct((tokens, cols), jnp.float32)] * 3,
        in_specs=[smem()] * 4 + [pl.BlockSpec((tokens, cols), lambda p: (0, group)), vmem(), vmem()],
        out_specs=[vmem()] * 3,
        scratch_shapes=[pltpu.VMEM((2 * tokens, 2 * HEAD_SIZE), queries.dtype)],
        compiler_params=pltpu.CompilerParams(vmem_limit_bytes=16 << 20),
        cost_estimate=pl.CostEstimate(
            flops=4 * tokens * cols * 640 * 3, transcendentals=tokens * heads * 640, bytes_accessed=4 * tokens * cols
        ),
    )(*scalars, queries, prev, local)


def far_body(
    offsets_ref, unions, picks, counts, q_ref, sum_ref, peak_ref, total_ref, prev_ref, same_ref, other_ref, out_ref, far,
    *, group, heads, per_dev, owners,
):
    rank = lax.axis_index("ctx")
    vper, union = picks.shape[2], unions.shape[2]
    hops = owners // 2 - 1
    slots = [(None, 0, j) for j in range(vper)]
    slots += [(k, side, j) for k in range(hops) for side in range(2) for j in range(vper)]
    extra = len(slots) % 2
    slots += [slots[-1]] * extra
    lane = lax.broadcasted_iota(jnp.int32, (1, PAIR), 1)
    block_row = lax.broadcasted_iota(jnp.int32, (per_dev, PAIR), 0)

    hides = []
    for i in range(heads):
        head = group * heads + i
        goods = []
        for at, slot in enumerate(slots):
            k, side, j = slot
            owner = rank - 1 if k is None else (rank ^ 1 if side else rank) - 2 * (k + 1)
            good = (owner >= 0) & (owner <= rank - (1 if k is None else 2))
            owner = jnp.maximum(owner, 0)
            entry, used = picked(picks, counts, head, owner, j)
            good = good & used
            if extra and at == len(slots) - 1:
                good = good & False
            if k is None:
                source = prev_ref
                block = unions[group, owner, entry]
                distance = block_row + (per_dev - block)
                seen = jnp.full((per_dev, PAIR), 1.0)
                for s in range(offsets_ref.shape[1]):
                    seen = jnp.where(distance == offsets_ref[head, s], 0.0, seen)
                bias = jnp.where(seen * jnp.where(good, 1.0, 0.0) > 0.5, 0.0, HIDE)
                start = block * BLOCK
            else:
                source = other_ref if side else same_ref
                bias = jnp.where(good, 0.0, HIDE).astype(jnp.float32)
                start = (k * union + entry) * BLOCK
            goods.append(bias)
            far[i, pl.ds(at * BLOCK, BLOCK), :] = source[pl.ds(pl.multiple_of(start, BLOCK), BLOCK), :]
        masks = []
        for tile in range(len(slots) // 2):
            mask = jnp.where(lane < BLOCK, goods[2 * tile], goods[2 * tile + 1])
            if mask.shape[0] > 1:
                mask = jnp.concatenate(
                    [jnp.broadcast_to(mask[r : r + 1], (BLOCK, PAIR)) for r in range(per_dev)], axis=0
                )
            masks.append(mask)
        hides.append(masks)

    def scores_of(i):
        return lax.dot_general(
            q_ref[:, i * HEAD_SIZE : (i + 1) * HEAD_SIZE], far[i, :, :HEAD_SIZE], CONTRACT,
            preferred_element_type=jnp.float32,
        )

    ahead = scores_of(0)
    for i in range(heads):
        cols = slice(i * HEAD_SIZE, (i + 1) * HEAD_SIZE)
        scores = ahead
        if i + 1 < heads:
            ahead = scores_of(i + 1)
        tiles = [scores[:, t * PAIR : (t + 1) * PAIR] + mask for t, mask in enumerate(hides[i])]
        before = peak_ref[:, cols]
        highest = functools.reduce(jnp.maximum, tiles)
        peak = jnp.maximum(jnp.max(highest, axis=1, keepdims=True), before)
        weights = [jnp.exp2((tile - peak) * SCALE2) for tile in tiles]
        keep = jnp.exp2((before - peak) * SCALE2)
        total = jnp.sum(functools.reduce(jnp.add, weights), axis=1, keepdims=True) + keep * total_ref[:, cols]
        numer = jnp.dot(
            jnp.concatenate([w.astype(jnp.bfloat16) for w in weights], axis=1), far[i, :, HEAD_SIZE:],
            preferred_element_type=jnp.float32,
        )
        out_ref[:, cols] = ((numer + keep * sum_ref[:, cols]) / total).astype(out_ref.dtype)


def attend_far(scalars, queries, sums, peaks, totals, prev, same, other, group, heads, owners):
    tokens = queries.shape[0]
    cols = heads * HEAD_SIZE
    slots = (owners - 1) * scalars[2].shape[2]
    slots += slots % 2
    per_dev = tokens // BLOCK
    return pl.pallas_call(
        functools.partial(far_body, group=group, heads=heads, per_dev=per_dev, owners=owners),
        grid=(1,),
        out_shape=jax.ShapeDtypeStruct((tokens, cols), queries.dtype),
        in_specs=[smem()] * 4 + [pl.BlockSpec((tokens, cols), lambda p: (0, group))] + [vmem()] * 6,
        out_specs=vmem(),
        scratch_shapes=[
            pltpu.VMEM((heads, slots * BLOCK, 2 * HEAD_SIZE), queries.dtype),
        ],
        compiler_params=pltpu.CompilerParams(vmem_limit_bytes=24 << 20),
        cost_estimate=pl.CostEstimate(
            flops=4 * tokens * cols * 512 * 3, transcendentals=tokens * heads * 512, bytes_accessed=4 * tokens * cols
        ),
    )(*scalars, queries, sums, peaks, totals, prev, same, other)


def project_body(*refs, spots, has_sum, groups):
    count = len(spots)
    ins, weight = refs[:count], refs[count]
    out = refs[-1]
    seat, members = lax.axis_index("head"), lax.axis_size("head")
    depth = ins[0].shape[1]
    total = refs[count + 1][...] if has_sum else None
    for x, (flip, by, g) in zip(ins, spots):
        source = lax.rem((seat ^ 1 if flip else seat) + members - by, members)
        start = pl.multiple_of((source * groups + g) * depth, depth)
        part = jnp.dot(x[...], weight[pl.ds(start, depth), :], preferred_element_type=jnp.float32)
        total = part if total is None else total + part
    out[...] = total.astype(out.dtype)


def project(ins, spots, weight, sums, dtype, groups):
    tokens, depth = ins[0].shape
    cols = weight.shape[1]
    args = list(ins) + [weight] + ([] if sums is None else [sums])
    return pl.pallas_call(
        functools.partial(project_body, spots=spots, has_sum=sums is not None, groups=groups),
        in_specs=[vmem()] * len(args),
        out_specs=vmem(),
        out_shape=jax.ShapeDtypeStruct((tokens, cols), dtype),
        compiler_params=pltpu.CompilerParams(vmem_limit_bytes=24 << 20),
        cost_estimate=pl.CostEstimate(
            flops=2 * tokens * cols * depth * len(ins) * 2, transcendentals=0, bytes_accessed=2 * depth * cols * len(ins)
        ),
    )(*args)


def turn(array, axis, by):
    size = lax.axis_size(axis)
    return lax.ppermute(array, axis, [(i, (i + by) % size) for i in range(size)])


def onward(array, axis, by):
    size = lax.axis_size(axis)
    return lax.ppermute(array, axis, [(i, i + by) for i in range(size - by)])


def swap(array, axis):
    size = lax.axis_size(axis)
    return lax.ppermute(array, axis, [(i, i ^ 1) for i in range(size)])


def shards(
    queries, key_rows, value_rows, slash_offsets, union_blocks, head_picks, owner_counts, out_weight
):
    groups = key_rows.shape[1] // HEAD_SIZE
    owners, members = lax.axis_size("ctx"), lax.axis_size("head")
    heads = slash_offsets.shape[0] // groups
    scalars = (slash_offsets, union_blocks, head_picks, owner_counts)
    made = prep(union_blocks, key_rows, value_rows, groups, union_blocks.shape[2])
    joined, blocks = made[:groups], made[groups]
    hops = owners // 2 - 1
    prevs, near, sames, others = [], [], [], []
    arrived = []
    for k in reversed(range(hops)):
        arrived.append(onward(blocks, "ctx", 2 * (k + 1)))
    span = blocks.shape[0] // groups
    for g in range(groups):
        rows = slice(g * span, (g + 1) * span)
        prevs.append(onward(joined[g], "ctx", 1))
        if hops > 0:
            sames.append(jnp.concatenate([part[rows] for part in arrived[::-1]], axis=0))
            others.append(swap(sames[g], "ctx"))
        else:
            sames.append(blocks[rows])
            others.append(blocks[rows])
    for g in range(groups):
        near.append(attend_near(scalars, queries, prevs[g], joined[g], g, heads))
    done, mates = [], []
    for g in range(groups):
        done.append(attend_far(scalars, queries, *near[g], prevs[g], sames[g], others[g], g, heads, owners))
        mates.append(swap(done[g], "head"))
    sums = None
    crossed = []
    for by in range(2, members, 2):
        for g in range(groups):
            here = turn(done[g], "head", by)
            crossed.append((here, swap(here, "head"), by, g))
    for g in range(groups):
        only = not crossed and g == groups - 1
        sums = project(
            [done[g], mates[g]], [(False, 0, g), (True, 0, g)], out_weight, sums,
            jnp.bfloat16 if only else jnp.float32, groups,
        )
    for at, (here, there, by, g) in enumerate(crossed):
        last = at == len(crossed) - 1
        sums = project([here], [(False, by, g)], out_weight, sums, jnp.float32, groups)
        sums = project([there], [(True, by, g)], out_weight, sums, jnp.bfloat16 if last else jnp.float32, groups)
    return sums


def solution(mesh):
    in_specs = (
        P("ctx", "head"),
        P("ctx", "head"),
        P("ctx", "head"),
        P("head", None),
        P("head", None, None),
        P("head", None, None),
        P("head", None),
        P(None, "head"),
    )
    return jax.shard_map(shards, mesh=mesh, in_specs=in_specs, out_specs=P("ctx", "head"), check_vma=False)
```

time: 216 us -> 70.4 us (0.33)
  the two profiles are of different devices: /device:TPU:0 before, /device:TPU:21 now
where the time goes in v1:
time: 70.4 us; the launch traced here: 70 us
  waiting for transfers between devices  23.7 us (34%)
  Pallas kernels  21.1 us (30%)
  starting transfers between devices  20.8 us (30%)
  local copies, waits for them, and re-layouts  4.28 us (6%)
    ppermute x2, waiting for transfers between devices, turn(): lax.ppermute(array, axis, [(i, (i + by) % size) for i in range(size)])  13.3 us
    ppermute x5, waiting for transfers between devices, onward(): return lax.ppermute(array, axis, [(i, i + by) for i in range(size - by)])  10.3 us
    ppermute x5, starting transfers between devices, onward(): return lax.ppermute(array, axis, [(i, i + by) for i in range(size - by)])  10.2 us
    ppermute x6, starting transfers between devices, swap(): return lax.ppermute(array, axis, [(i, i ^ 1) for i in range(size)])  8.96 us
    pallas_call x2, Pallas kernels, attend_near(): pl.pallas_call(functools.partial(near_body, group=group, heads=heads, per...  7.25 us
    pallas_call x2, Pallas kernels, attend_far(): pl.pallas_call(functools.partial(far_body, group=group, heads=heads, per_...  6.65 us
    pallas_call x6, Pallas kernels, project(): pl.pallas_call(functools.partial(project_body, spots=spots, has_sum=sums...  6.39 us
    unnamed x15, local copies, waits for them, and re-layouts  4.25 us
  transfers between devices with their start and end apart: 13, of which 4 were waited for; matrix products, arithmetic and copies ran while one was open for 2% of the time, Pallas kernels for 27%

profile of v1, /device:TPU:21, one launch (start us, length us, event | category | flops | bytes accessed | tf_op | source)
XLA Modules:
  0.0 70.0 jit_solution(13971868752505519294)
XLA Ops:
  0.0 0.0 copy-start.3
  0.0 0.8 %copy.14.unions = s32[2,8,2]{2,1,0:T(8,128)S(1)} copy(s32[2,8,2]{1,2,0:T(2,128)} %param.12) | data formatting | bytes 256 | tf_op args[4]
  0.8 0.0 copy-start
  0.8 0.9 %copy-done = bf16[512,256]{1,0:T(8,128)(2,1)S(1)} copy-done((bf16[512,256]{1,0:T(8,128)(2,1)S(1)}, bf16[512,256]{1,0:T(8,128)(2,1)}, u32[]{:S(2)}) %copy-start) | copy-done | bytes 262168
  1.7 0.0 copy-start.1
  1.7 0.9 %copy-done.1 = bf16[512,256]{1,0:T(8,128)(2,1)S(1)} copy-done((bf16[512,256]{1,0:T(8,128)(2,1)S(1)}, bf16[512,256]{1,0:T(8,128)(2,1)}, u32[]{:S(2)}) %copy-start.1) | copy-done | bytes 262168
  2.7 0.0 copy-start.2
  2.7 0.8 %prep.1 = (bf16[512,256]{1,0:T(8,128)(2,1)S(1)}, bf16[512,256]{1,0:T(8,128)(2,1)S(1)}, bf16[256,256]{1,0:T(8,128)(2,1)S(1)}) custom-call(s32[2,8,2]{2,1,0:T(8,128)S(1)} %copy.14.unions, bf16[512,256]{1,0:T(8,128)(2,1)S(1)} %copy-done, bf16[512,256]{1,0:T(8,128)(2,1)S(1)} %copy-done.1), custom_call_target="tpu_custom_call" | custom-call | tf_op jit(solution)/shard_map/prep/pallas_call | solution.py:45
  3.5 3.2 %collective-permute-start.1 = (bf16[256,256]{1,0:T(8,128)(2,1)S(1)}, bf16[256,256]{1,0:T(8,128)(2,1)S(1)}, u32[]{:S(2)}, u32[]{:S(2)}) collective-permute-start(bf16[256,256]{1,0:T(8,128)(2,1)S(1)} %get-tuple-element.18), channel_id=1, source_target_pairs={{0,8},{4,12},{8,16},{12,20},{16,24},{20,28},{1,9},{5,13},{9,17},{1... | collective-permute-start | bytes 393224 | tf_op jit(solution)/shard_map/ppermute | solution.py:292
  6.7 1.3 %collective-permute-start.2 = (bf16[256,256]{1,0:T(8,128)(2,1)S(1)}, bf16[256,256]{1,0:T(8,128)(2,1)S(1)}, u32[]{:S(2)}, u32[]{:S(2)}) collective-permute-start(bf16[256,256]{1,0:T(8,128)(2,1)S(1)} %get-tuple-element.18), channel_id=1, source_target_pairs={{0,16},{4,20},{8,24},{12,28},{1,17},{5,21},{9,25},{13,29},{2,18},{... | collective-permute-start | bytes 393224 | tf_op jit(solution)/shard_map/ppermute | solution.py:292
  8.0 0.7 collective-permute-start.3
  8.7 3.1 %collective-permute-start.7 = (bf16[512,256]{1,0:T(8,128)(2,1)S(1)}, bf16[512,256]{1,0:T(8,128)(2,1)S(1)}, u32[]{:S(2)}, u32[]{:S(2)}) collective-permute-start(bf16[512,256]{1,0:T(8,128)(2,1)S(1)} %get-tuple-element.19.local_ref), channel_id=1, source_target_pairs={{0,4},{4,8},{8,12},{12,16},{16,20},{20,24},{24,28},{1,5},{5,9},{9,... | collective-permute-start | bytes 786440 | tf_op jit(solution)/shard_map/ppermute | solution.py:292
  11.8 1.9 %collective-permute-start = (bf16[512,256]{1,0:T(8,128)(2,1)S(1)}, bf16[512,256]{1,0:T(8,128)(2,1)S(1)}, u32[]{:S(2)}, u32[]{:S(2)}) collective-permute-start(bf16[512,256]{1,0:T(8,128)(2,1)S(1)} %get-tuple-element.14.local_ref), channel_id=1, source_target_pairs={{0,4},{4,8},{8,12},{12,16},{16,20},{20,24},{24,28},{1,5},{5,9},{9,... | collective-permute-start | bytes 786440 | tf_op jit(solution)/shard_map/ppermute | solution.py:292
  13.7 0.8 %copy.15.picks = s32[8,8,1]{2,1,0:T(8,128)S(1)} copy(s32[8,8,1]{1,2,0:T(1,128)} %param.13) | data formatting | bytes 512 | tf_op args[5]
  14.5 0.8 %copy.13.offsets_ref = s32[8,4]{1,0:T(8,128)S(1)} copy(s32[8,4]{0,1:T(4,128)} %param.11) | data formatting | bytes 256 | tf_op args[3]
  15.3 0.0 collective-permute-done.1
  15.3 0.0 collective-permute-done.2
  15.3 0.0 collective-permute-done.3
  15.4 1.2 %collective-permute-start.8 = (bf16[384,256]{1,0:T(8,128)(2,1)S(1)}, bf16[384,256]{1,0:T(8,128)(2,1)S(1)}, u32[]{:S(2)}, u32[]{:S(2)}) collective-permute-start(bf16[384,256]{1,0:T(8,128)(2,1)S(1)} %pad_maximum_fusion.1.same_ref), channel_id=1, source_target_pairs={{0,4},{4,0},{8,12},{12,8},{16,20},{20,16},{24,28},{28,24},{1,5},{5... | collective-permute-start | bytes 589832 | tf_op jit(solution)/shard_map/ppermute | solution.py:297
  16.6 0.4 collective-permute-start.4
  17.0 8.3 %collective-permute-done.7.prev_ref = bf16[512,256]{1,0:T(8,128)(2,1)S(1)} collective-permute-done((bf16[512,256]{1,0:T(8,128)(2,1)S(1)}, bf16[512,256]{1,0:T(8,128)(2,1)S(1)}, u32[]{:S(2)}, u32[]{:S(2)}) %collective-permute-start.7) | collective-permute-done | bytes 262176 | tf_op jit(solution)/shard_map/ppermute | solution.py:292
  25.3 0.0 copy-done.3
  25.3 0.0 copy-done.2
  25.3 3.6 %shard_map.84 = (f32[512,512]{1,0:T(8,128)S(1)}, f32[512,512]{1,0:T(8,128)S(1)}, f32[512,512]{1,0:T(8,128)S(1)}) custom-call(s32[8,4]{1,0:T(8,128)S(1)} %copy.13.offsets_ref, s32[2,8,2]{2,1,0:T(8,128)S(1)} %copy.14.unions, s32[8,8,1]{2,1,0:T(8,128)S(1)} %copy.15.picks, s32[8,8]{1,0:T(8,128)S(1)} %copy-done.3, bf16[512,1024]{1,0:T(8,128)(2,1)S(1)} %copy-done.2, ...), custom_call_target="tpu_custom_call" | custom-call | flops 2013265920 | bytes 1048576 | tf_op jit(solution)/shard_map/pallas_call | solution.py:140
  28.9 2.0 %collective-permute-done.prev_ref = bf16[512,256]{1,0:T(8,128)(2,1)S(1)} collective-permute-done((bf16[512,256]{1,0:T(8,128)(2,1)S(1)}, bf16[512,256]{1,0:T(8,128)(2,1)S(1)}, u32[]{:S(2)}, u32[]{:S(2)}) %collective-permute-start) | collective-permute-done | bytes 262176 | tf_op jit(solution)/shard_map/ppermute | solution.py:292
  30.9 0.0 slice-start
  30.9 3.6 %shard_map.82 = (f32[512,512]{1,0:T(8,128)S(1)}, f32[512,512]{1,0:T(8,128)S(1)}, f32[512,512]{1,0:T(8,128)S(1)}) custom-call(s32[8,4]{1,0:T(8,128)S(1)} %copy.13.offsets_ref, s32[2,8,2]{2,1,0:T(8,128)S(1)} %copy.14.unions, s32[8,8,1]{2,1,0:T(8,128)S(1)} %copy.15.picks, s32[8,8]{1,0:T(8,128)S(1)} %copy-done.3, bf16[512,1024]{1,0:T(8,128)(2,1)S(1)} %copy-done.2, ...), custom_call_target="tpu_custom_call" | custom-call | flops 2013265920 | bytes 1048576 | tf_op jit(solution)/shard_map/pallas_call | solution.py:140
  34.6 0.0 collective-permute-done.8.other_ref
  34.6 0.0 slice-start.1
  34.6 3.3 %shard_map.85.refs_0_ = bf16[512,512]{1,0:T(8,128)(2,1)S(1)} custom-call(s32[8,4]{1,0:T(8,128)S(1)} %copy.13.offsets_ref, s32[2,8,2]{2,1,0:T(8,128)S(1)} %copy.14.unions, s32[8,8,1]{2,1,0:T(8,128)S(1)} %copy.15.picks, s32[8,8]{1,0:T(8,128)S(1)} %copy-done.3, bf16[512,1024]{1,0:T(8,128)(2,1)S(1)} %copy-done.2, f32[512,512]{1,0:T(8,128)S(1)} %get-tuple-element.20.sum_ref, ...), custom_call_target="tpu_custom_call" | custom-call | flops 1610612736 | bytes 1048576 | tf_op jit(solution)/shard_map/pallas_call | solution.py:238
  37.9 0.3 collective-permute-start.9
  38.2 0.0 collective-permute-done.4.other_ref
  38.2 3.3 %shard_map.83.refs_0_ = bf16[512,512]{1,0:T(8,128)(2,1)S(1)} custom-call(s32[8,4]{1,0:T(8,128)S(1)} %copy.13.offsets_ref, s32[2,8,2]{2,1,0:T(8,128)S(1)} %copy.14.unions, s32[8,8,1]{2,1,0:T(8,128)S(1)} %copy.15.picks, s32[8,8]{1,0:T(8,128)S(1)} %copy-done.3, bf16[512,1024]{1,0:T(8,128)(2,1)S(1)} %copy-done.2, f32[512,512]{1,0:T(8,128)S(1)} %get-tuple-element.15.sum_ref, ...), custom_call_target="tpu_custom_call" | custom-call | flops 1610612736 | bytes 1048576 | tf_op jit(solution)/shard_map/pallas_call | solution.py:238
  41.5 1.3 %collective-permute-start.5 = (bf16[512,512]{1,0:T(8,128)(2,1)S(1)}, bf16[512,512]{1,0:T(8,128)(2,1)S(1)}, u32[]{:S(2)}, u32[]{:S(2)}) collective-permute-start(bf16[512,512]{1,0:T(8,128)(2,1)S(1)} %shard_map.83.refs_0_), channel_id=1, source_target_pairs={{0,2},{1,3},{2,0},{3,1},{4,6},{5,7},{6,4},{7,5},{8,10},{9,11},{10,... | collective-permute-start | bytes 1572872 | tf_op jit(solution)/shard_map/ppermute | solution.py:287
  42.8 1.7 %collective-permute-start.12 = (bf16[512,512]{1,0:T(8,128)(2,1)S(1)}, bf16[512,512]{1,0:T(8,128)(2,1)S(1)}, u32[]{:S(2)}, u32[]{:S(2)}) collective-permute-start(bf16[512,512]{1,0:T(8,128)(2,1)S(1)} %shard_map.85.refs_0_), channel_id=1, source_target_pairs={{0,1},{1,0},{2,3},{3,2},{4,5},{5,4},{6,7},{7,6},{8,9},{9,8},{10,11... | collective-permute-start | bytes 1572872 | tf_op jit(solution)/shard_map/ppermute | solution.py:297
  44.6 0.0 collective-permute-start.11
  44.6 5.7 %collective-permute-done.9.refs_0_ = bf16[512,512]{1,0:T(8,128)(2,1)S(1)} collective-permute-done((bf16[512,512]{1,0:T(8,128)(2,1)S(1)}, bf16[512,512]{1,0:T(8,128)(2,1)S(1)}, u32[]{:S(2)}, u32[]{:S(2)}) %collective-permute-start.9) | collective-permute-done | bytes 524320 | tf_op jit(solution)/shard_map/ppermute | solution.py:287
  50.3 3.6 %collective-permute-start.10 = (bf16[512,512]{1,0:T(8,128)(2,1)S(1)}, bf16[512,512]{1,0:T(8,128)(2,1)S(1)}, u32[]{:S(2)}, u32[]{:S(2)}) collective-permute-start(bf16[512,512]{1,0:T(8,128)(2,1)S(1)} %collective-permute-done.9.refs_0_), channel_id=1, source_target_pairs={{0,1},{1,0},{2,3},{3,2},{4,5},{5,4},{6,7},{7,6},{8,9},{9,8},{10,11... | collective-permute-start | bytes 1572872 | tf_op jit(solution)/shard_map/ppermute | solution.py:297
  53.9 7.6 %collective-permute-done.5.refs_0_ = bf16[512,512]{1,0:T(8,128)(2,1)S(1)} collective-permute-done((bf16[512,512]{1,0:T(8,128)(2,1)S(1)}, bf16[512,512]{1,0:T(8,128)(2,1)S(1)}, u32[]{:S(2)}, u32[]{:S(2)}) %collective-permute-start.5) | collective-permute-done | bytes 524320 | tf_op jit(solution)/shard_map/ppermute | solution.py:287
  61.5 2.0 %collective-permute-start.6 = (bf16[512,512]{1,0:T(8,128)(2,1)S(1)}, bf16[512,512]{1,0:T(8,128)(2,1)S(1)}, u32[]{:S(2)}, u32[]{:S(2)}) collective-permute-start(bf16[512,512]{1,0:T(8,128)(2,1)S(1)} %collective-permute-done.5.refs_0_), channel_id=1, source_target_pairs={{0,1},{1,0},{2,3},{3,2},{4,5},{5,4},{6,7},{7,6},{8,9},{9,8},{10,11... | collective-permute-start | bytes 1572872 | tf_op jit(solution)/shard_map/ppermute | solution.py:297
  63.5 0.0 collective-permute-done.12.refs_1_
  63.5 0.0 slice-done
  63.6 0.0 slice-done.1
  63.6 1.3 %shard_map.86.refs_3_ = f32[512,1024]{1,0:T(8,128)S(1)} custom-call(bf16[512,512]{1,0:T(8,128)(2,1)S(1)} %shard_map.85.refs_0_, bf16[512,512]{1,0:T(8,128)(2,1)S(1)} %collective-permute-done.12.refs_1_, bf16[4096,1024]{1,0:T(8,128)(2,1)S(1)} %bitcast.1), custom_call_target="tpu_custom_call" | custom-call | flops 2147483648 | bytes 2097152 | tf_op jit(solution)/shard_map/pallas_call | solution.py:273
  64.8 0.0 collective-permute-done.11.refs_1_
  64.8 1.3 %shard_map.87.refs_2_ = f32[512,1024]{1,0:T(8,128)S(1)} custom-call(bf16[512,512]{1,0:T(8,128)(2,1)S(1)} %shard_map.83.refs_0_, bf16[512,512]{1,0:T(8,128)(2,1)S(1)} %collective-permute-done.11.refs_1_, bf16[4096,1024]{1,0:T(8,128)(2,1)S(1)} %bitcast.1, f32[512,1024]{1,0:T(8,128)S(1)} %shard_map.86.refs_3_), custom_call_target="tpu_custom_call" | custom-call | flops 2147483648 | bytes 2097152 | tf_op jit(solution)/shard_map/pallas_call | solution.py:273
  66.1 0.7 %shard_map.88.refs_2_ = f32[512,1024]{1,0:T(8,128)S(1)} custom-call(bf16[512,512]{1,0:T(8,128)(2,1)S(1)} %collective-permute-done.9.refs_0_, bf16[4096,1024]{1,0:T(8,128)(2,1)S(1)} %bitcast.1, f32[512,1024]{1,0:T(8,128)S(1)} %shard_map.87.refs_2_), custom_call_target="tpu_custom_call" | custom-call | flops 1073741824 | bytes 1048576 | tf_op jit(solution)/shard_map/pallas_call | solution.py:273
  66.8 0.0 collective-permute-done.10.refs_0_
  66.8 0.7 %shard_map.89.refs_2_ = f32[512,1024]{1,0:T(8,128)S(1)} custom-call(bf16[512,512]{1,0:T(8,128)(2,1)S(1)} %collective-permute-done.10.refs_0_, bf16[4096,1024]{1,0:T(8,128)(2,1)S(1)} %bitcast.1, f32[512,1024]{1,0:T(8,128)S(1)} %shard_map.88.refs_2_), custom_call_target="tpu_custom_call" | custom-call | flops 1073741824 | bytes 1048576 | tf_op jit(solution)/shard_map/pallas_call | solution.py:273
  67.6 0.7 %shard_map.90.refs_2_ = f32[512,1024]{1,0:T(8,128)S(1)} custom-call(bf16[512,512]{1,0:T(8,128)(2,1)S(1)} %collective-permute-done.5.refs_0_, bf16[4096,1024]{1,0:T(8,128)(2,1)S(1)} %bitcast.1, f32[512,1024]{1,0:T(8,128)S(1)} %shard_map.89.refs_2_), custom_call_target="tpu_custom_call" | custom-call | flops 1073741824 | bytes 1048576 | tf_op jit(solution)/shard_map/pallas_call | solution.py:273
  68.3 0.0 collective-permute-done.6.refs_0_
  68.3 1.7 %shard_map.91 = bf16[512,1024]{1,0:T(8,128)(2,1)} custom-call(bf16[512,512]{1,0:T(8,128)(2,1)S(1)} %collective-permute-done.6.refs_0_, bf16[4096,1024]{1,0:T(8,128)(2,1)S(1)} %bitcast.1, f32[512,1024]{1,0:T(8,128)S(1)} %shard_map.90.refs_2_), custom_call_target="tpu_custom_call" | custom-call | flops 1073741824 | bytes 1048576 | tf_op jit(solution)/shard_map/pallas_call | solution.py:273
  (6 shorter events, 0.1 us)
Async XLA Ops:
  0.0 25.3 %copy-start.3 = (s32[8,8]{1,0:T(8,128)S(1)}, s32[8,8]{1,0:T(8,128)}, u32[]{:S(2)}) copy-start(s32[8,8]{1,0:T(8,128)} %counts.7) | copy-start | bytes 772
  0.8 0.9 %copy-start = (bf16[512,256]{1,0:T(8,128)(2,1)S(1)}, bf16[512,256]{1,0:T(8,128)(2,1)}, u32[]{:S(2)}) copy-start(bf16[512,256]{1,0:T(8,128)(2,1)} %keys.1) | copy-start | bytes 786436
  1.7 0.9 %copy-start.1 = (bf16[512,256]{1,0:T(8,128)(2,1)S(1)}, bf16[512,256]{1,0:T(8,128)(2,1)}, u32[]{:S(2)}) copy-start(bf16[512,256]{1,0:T(8,128)(2,1)} %values.1) | copy-start | bytes 786436
  2.7 22.6 %copy-start.2 = (bf16[512,1024]{1,0:T(8,128)(2,1)S(1)}, bf16[512,1024]{1,0:T(8,128)(2,1)}, u32[]{:S(2)}) copy-start(bf16[512,1024]{1,0:T(8,128)(2,1)} %q_ref.7) | copy-start | bytes 3145732
  3.5 11.8 %collective-permute-start.1 = (bf16[256,256]{1,0:T(8,128)(2,1)S(1)}, bf16[256,256]{1,0:T(8,128)(2,1)S(1)}, u32[]{:S(2)}, u32[]{:S(2)}) collective-permute-start(bf16[256,256]{1,0:T(8,128)(2,1)S(1)} %get-tuple-element.18), channel_id=1, source_target_pairs={{0,8},{4,12},{8,16},{12,20},{16,24},{20,28},{1,9},{5,13},{9,17},{1... | collective-permute-start | bytes 393224 | tf_op jit(solution)/shard_map/ppermute | solution.py:292
  6.7 8.6 %collective-permute-start.2 = (bf16[256,256]{1,0:T(8,128)(2,1)S(1)}, bf16[256,256]{1,0:T(8,128)(2,1)S(1)}, u32[]{:S(2)}, u32[]{:S(2)}) collective-permute-start(bf16[256,256]{1,0:T(8,128)(2,1)S(1)} %get-tuple-element.18), channel_id=1, source_target_pairs={{0,16},{4,20},{8,24},{12,28},{1,17},{5,21},{9,25},{13,29},{2,18},{... | collective-permute-start | bytes 393224 | tf_op jit(solution)/shard_map/ppermute | solution.py:292
  8.0 7.3 %collective-permute-start.3 = (bf16[256,256]{1,0:T(8,128)(2,1)S(1)}, bf16[256,256]{1,0:T(8,128)(2,1)S(1)}, u32[]{:S(2)}, u32[]{:S(2)}) collective-permute-start(bf16[256,256]{1,0:T(8,128)(2,1)S(1)} %get-tuple-element.18), channel_id=1, source_target_pairs={{0,24},{4,28},{1,25},{5,29},{2,26},{6,30},{3,27},{7,31}} | collective-permute-start | bytes 393224 | tf_op jit(solution)/shard_map/ppermute | solution.py:292
  8.7 16.6 %collective-permute-start.7 = (bf16[512,256]{1,0:T(8,128)(2,1)S(1)}, bf16[512,256]{1,0:T(8,128)(2,1)S(1)}, u32[]{:S(2)}, u32[]{:S(2)}) collective-permute-start(bf16[512,256]{1,0:T(8,128)(2,1)S(1)} %get-tuple-element.19.local_ref), channel_id=1, source_target_pairs={{0,4},{4,8},{8,12},{12,16},{16,20},{20,24},{24,28},{1,5},{5,9},{9,... | collective-permute-start | bytes 786440 | tf_op jit(solution)/shard_map/ppermute | solution.py:292
  11.8 19.1 %collective-permute-start = (bf16[512,256]{1,0:T(8,128)(2,1)S(1)}, bf16[512,256]{1,0:T(8,128)(2,1)S(1)}, u32[]{:S(2)}, u32[]{:S(2)}) collective-permute-start(bf16[512,256]{1,0:T(8,128)(2,1)S(1)} %get-tuple-element.14.local_ref), channel_id=1, source_target_pairs={{0,4},{4,8},{8,12},{12,16},{16,20},{20,24},{24,28},{1,5},{5,9},{9,... | collective-permute-start | bytes 786440 | tf_op jit(solution)/shard_map/ppermute | solution.py:292
  15.4 19.2 %collective-permute-start.8 = (bf16[384,256]{1,0:T(8,128)(2,1)S(1)}, bf16[384,256]{1,0:T(8,128)(2,1)S(1)}, u32[]{:S(2)}, u32[]{:S(2)}) collective-permute-start(bf16[384,256]{1,0:T(8,128)(2,1)S(1)} %pad_maximum_fusion.1.same_ref), channel_id=1, source_target_pairs={{0,4},{4,0},{8,12},{12,8},{16,20},{20,16},{24,28},{28,24},{1,5},{5... | collective-permute-start | bytes 589832 | tf_op jit(solution)/shard_map/ppermute | solution.py:297
  16.6 21.6 %collective-permute-start.4 = (bf16[384,256]{1,0:T(8,128)(2,1)S(1)}, bf16[384,256]{1,0:T(8,128)(2,1)S(1)}, u32[]{:S(2)}, u32[]{:S(2)}) collective-permute-start(bf16[384,256]{1,0:T(8,128)(2,1)S(1)} %pad_maximum_fusion.same_ref), channel_id=1, source_target_pairs={{0,4},{4,0},{8,12},{12,8},{16,20},{20,16},{24,28},{28,24},{1,5},{5... | collective-permute-start | bytes 589832 | tf_op jit(solution)/shard_map/ppermute | solution.py:297
  30.9 32.6 %slice-start = ((s8[8388608]{0:T(1024)(128)(4,1)}), s8[4194304]{0:T(1024)(128)(4,1)S(1)}, s32[]{:S(2)}) async-start(s8[8388608]{0:T(1024)(128)(4,1)} %bitcast), calls=%async_computation | async-start | bytes 8388608
  34.6 29.0 %slice-start.1 = ((s8[8388608]{0:T(1024)(128)(4,1)}), s8[4194304]{0:T(1024)(128)(4,1)S(1)}, s32[]{:S(2)}) async-start(s8[8388608]{0:T(1024)(128)(4,1)} %bitcast), calls=%async_computation.1 | async-start | bytes 8388608
  37.9 12.4 %collective-permute-start.9 = (bf16[512,512]{1,0:T(8,128)(2,1)S(1)}, bf16[512,512]{1,0:T(8,128)(2,1)S(1)}, u32[]{:S(2)}, u32[]{:S(2)}) collective-permute-start(bf16[512,512]{1,0:T(8,128)(2,1)S(1)} %shard_map.85.refs_0_), channel_id=1, source_target_pairs={{0,2},{1,3},{2,0},{3,1},{4,6},{5,7},{6,4},{7,5},{8,10},{9,11},{10,... | collective-permute-start | bytes 1572872 | tf_op jit(solution)/shard_map/ppermute | solution.py:287
  41.5 20.0 %collective-permute-start.5 = (bf16[512,512]{1,0:T(8,128)(2,1)S(1)}, bf16[512,512]{1,0:T(8,128)(2,1)S(1)}, u32[]{:S(2)}, u32[]{:S(2)}) collective-permute-start(bf16[512,512]{1,0:T(8,128)(2,1)S(1)} %shard_map.83.refs_0_), channel_id=1, source_target_pairs={{0,2},{1,3},{2,0},{3,1},{4,6},{5,7},{6,4},{7,5},{8,10},{9,11},{10,... | collective-permute-start | bytes 1572872 | tf_op jit(solution)/shard_map/ppermute | solution.py:287
  42.8 20.7 %collective-permute-start.12 = (bf16[512,512]{1,0:T(8,128)(2,1)S(1)}, bf16[512,512]{1,0:T(8,128)(2,1)S(1)}, u32[]{:S(2)}, u32[]{:S(2)}) collective-permute-start(bf16[512,512]{1,0:T(8,128)(2,1)S(1)} %shard_map.85.refs_0_), channel_id=1, source_target_pairs={{0,1},{1,0},{2,3},{3,2},{4,5},{5,4},{6,7},{7,6},{8,9},{9,8},{10,11... | collective-permute-start | bytes 1572872 | tf_op jit(solution)/shard_map/ppermute | solution.py:297
  44.6 20.3 %collective-permute-start.11 = (bf16[512,512]{1,0:T(8,128)(2,1)S(1)}, bf16[512,512]{1,0:T(8,128)(2,1)S(1)}, u32[]{:S(2)}, u32[]{:S(2)}) collective-permute-start(bf16[512,512]{1,0:T(8,128)(2,1)S(1)} %shard_map.83.refs_0_), channel_id=1, source_target_pairs={{0,1},{1,0},{2,3},{3,2},{4,5},{5,4},{6,7},{7,6},{8,9},{9,8},{10,11... | collective-permute-start | bytes 1572872 | tf_op jit(solution)/shard_map/ppermute | solution.py:297
  50.3 16.5 %collective-permute-start.10 = (bf16[512,512]{1,0:T(8,128)(2,1)S(1)}, bf16[512,512]{1,0:T(8,128)(2,1)S(1)}, u32[]{:S(2)}, u32[]{:S(2)}) collective-permute-start(bf16[512,512]{1,0:T(8,128)(2,1)S(1)} %collective-permute-done.9.refs_0_), channel_id=1, source_target_pairs={{0,1},{1,0},{2,3},{3,2},{4,5},{5,4},{6,7},{7,6},{8,9},{9,8},{10,11... | collective-permute-start | bytes 1572872 | tf_op jit(solution)/shard_map/ppermute | solution.py:297
  61.5 6.8 %collective-permute-start.6 = (bf16[512,512]{1,0:T(8,128)(2,1)S(1)}, bf16[512,512]{1,0:T(8,128)(2,1)S(1)}, u32[]{:S(2)}, u32[]{:S(2)}) collective-permute-start(bf16[512,512]{1,0:T(8,128)(2,1)S(1)} %collective-permute-done.5.refs_0_), channel_id=1, source_target_pairs={{0,1},{1,0},{2,3},{3,2},{4,5},{5,4},{6,7},{7,6},{8,9},{9,8},{10,11... | collective-permute-start | bytes 1572872 | tf_op jit(solution)/shard_map/ppermute | solution.py:297

commit v2 on v1

--- a/solution.py
+++ b/solution.py
@@ -17,22 +17,42 @@
 CONTRACT = (((1,), (1,)), ((), ()))
 
 
-def prep_body(unions, keys, values, *outs, groups, union):
+def prep_body(unions_hbm, keys_hbm, values_hbm, *outs, groups, union):
+    *outs, unions, keys, values, sems = outs
+    loads = [
+        pltpu.make_async_copy(unions_hbm, unions, sems.at[2]),
+        pltpu.make_async_copy(keys_hbm, keys, sems.at[0]),
+        pltpu.make_async_copy(values_hbm, values, sems.at[1]),
+    ]
+    for load in loads:
+        load.start()
+    for load in loads:
+        load.wait()
     rank = lax.axis_index("ctx")
-    blocks = outs[groups]
     for g in range(groups):
+        blocks = outs[groups + g]
         cols = pl.ds(g * HEAD_SIZE, HEAD_SIZE)
         outs[g][:, :HEAD_SIZE] = keys[:, cols]
         outs[g][:, HEAD_SIZE:] = values[:, cols]
         for u in range(union):
-            start = pl.multiple_of(unions[g, rank, u] * BLOCK, BLOCK)
-            rows = pl.ds((g * union + u) * BLOCK, BLOCK)
-            blocks[rows, :HEAD_SIZE] = keys[pl.ds(start, BLOCK), cols]
-            blocks[rows, HEAD_SIZE:] = values[pl.ds(start, BLOCK), cols]
-
-
-def smem():
-    return pl.BlockSpec(memory_space=pltpu.SMEM)
+            start = pl.multiple_of(unions[g, u, rank] * BLOCK, BLOCK)
+            rows = pl.ds(u * BLOCK, BLOCK)
+            every = pl.ds((g * union + u) * BLOCK, BLOCK)
+            for block_out, at in ((blocks, rows), (outs[2 * groups], every)):
+                block_out[at, :HEAD_SIZE] = keys[pl.ds(start, BLOCK), cols]
+                block_out[at, HEAD_SIZE:] = values[pl.ds(start, BLOCK), cols]
+
+
+def hbm():
+    return pl.BlockSpec(memory_space=pltpu.HBM)
+
+
+def stay(array):
+    return pltpu.with_memory_space_constraint(array, pltpu.HBM)
+
+
+def small(arrays):
+    return [pltpu.SMEM(a.shape, a.dtype) for a in arrays]
 
 
 def vmem():
@@ -45,26 +65,35 @@
     return pl.pallas_call(
         functools.partial(prep_body, groups=groups, union=union),
         out_shape=[jax.ShapeDtypeStruct((tokens, wide), keys.dtype)] * groups
+        + [jax.ShapeDtypeStruct((union * BLOCK, wide), keys.dtype)] * groups
         + [jax.ShapeDtypeStruct((groups * union * BLOCK, wide), keys.dtype)],
-        grid=(1,),
-        in_specs=[smem()] + [pl.BlockSpec(keys.shape, lambda p: (0, 0))] * 2,
-        out_specs=[vmem()] * (groups + 1),
+        in_specs=[hbm()] * 3,
+        out_specs=[vmem()] * (2 * groups + 1),
+        scratch_shapes=small([unions]) + [pltpu.VMEM(keys.shape, keys.dtype)] * 2 + [pltpu.SemaphoreType.DMA((3,))],
         compiler_params=pltpu.CompilerParams(vmem_limit_bytes=8 << 20),
         name="prep",
-    )(unions, keys, values)
+    )(stay(unions), stay(keys), stay(values))
 
 
 def picked(picks, counts, head, owner, j):
-    return picks[head, owner, j], j < counts[head, owner]
+    return picks[head, j, owner], j < counts[head, owner]
 
 
 def near_body(
-    offsets_ref, unions, picks, counts, q_ref, prev_ref, local_ref, sum_ref, peak_ref, total_ref, window,
+    offsets_hbm, unions_hbm, picks_hbm, counts_hbm, q_hbm, prev_ref, local_ref, sum_ref, peak_ref, total_ref, window,
+    q_ref, offsets_ref, unions, picks, counts, sem,
     *, group, heads, per_dev,
 ):
     rank = lax.axis_index("ctx")
     tokens = per_dev * BLOCK
     wide = (per_dev + 2) * BLOCK
+    width = heads * HEAD_SIZE
+    load = pltpu.make_async_copy(q_hbm.at[:, pl.ds(group * width, width)], q_ref, sem.at[4])
+    load.start()
+    tables = [(offsets_hbm, offsets_ref), (unions_hbm, unions), (picks_hbm, picks), (counts_hbm, counts)]
+    tables = [pltpu.make_async_copy(a, b, sem.at[i]) for i, (a, b) in enumerate(tables)]
+    for copy in tables:
+        copy.start()
     window[:tokens, :] = prev_ref[...]
     window[tokens:, :] = local_ref[...]
     place = lax.broadcasted_iota(jnp.int32, (1, wide), 1) // BLOCK
@@ -80,14 +109,16 @@
             preferred_element_type=jnp.float32,
         )
 
+    for copy in tables:
+        copy.wait()
     slashes, columns = [], []
     for i in range(heads):
         head = group * heads + i
-        slashes.append([offsets_ref[head, s] for s in range(offsets_ref.shape[1])])
+        slashes.append([offsets_ref[s, head] for s in range(offsets_ref.shape[0])])
         at = []
-        for j in range(picks.shape[2]):
+        for j in range(picks.shape[1]):
             entry, used = picked(picks, counts, head, rank, j)
-            at.append(jnp.where(used, unions[group, rank, entry] + per_dev, -tokens))
+            at.append(jnp.where(used, unions[group, entry, rank] + per_dev, -tokens))
         columns.append(at)
     seen_slash = []
     for i in range(heads):
@@ -99,6 +130,7 @@
             seen_slash.append((distance, jnp.where(seen, 0.0, HIDE)))
 
     steps = tokens // PAIR
+    load.wait()
     ahead = scores_of(0)
     for step in range(steps):
         near = ahead
@@ -139,32 +171,46 @@
     cols = heads * HEAD_SIZE
     return pl.pallas_call(
         functools.partial(near_body, group=group, heads=heads, per_dev=tokens // BLOCK),
-        grid=(1,),
         out_shape=[jax.ShapeDtypeStruct((tokens, cols), jnp.float32)] * 3,
-        in_specs=[smem()] * 4 + [pl.BlockSpec((tokens, cols), lambda p: (0, group)), vmem(), vmem()],
+        in_specs=[hbm()] * 5 + [vmem(), vmem()],
         out_specs=[vmem()] * 3,
-        scratch_shapes=[pltpu.VMEM((2 * tokens, 2 * HEAD_SIZE), queries.dtype)],
+        scratch_shapes=[
+            pltpu.VMEM((2 * tokens, 2 * HEAD_SIZE), queries.dtype),
+            pltpu.VMEM((tokens, cols), queries.dtype),
+            *small(scalars),
+            pltpu.SemaphoreType.DMA((5,)),
+        ],
         compiler_params=pltpu.CompilerParams(vmem_limit_bytes=16 << 20),
         cost_estimate=pl.CostEstimate(
             flops=4 * tokens * cols * 640 * 3, transcendentals=tokens * heads * 640, bytes_accessed=4 * tokens * cols
         ),
-    )(*scalars, queries, prev, local)
+    )(*[stay(a) for a in scalars], stay(queries), prev, local)
 
 
 def far_body(
-    offsets_ref, unions, picks, counts, q_ref, sum_ref, peak_ref, total_ref, prev_ref, same_ref, other_ref, out_ref, far,
+    offsets_hbm, unions_hbm, picks_hbm, counts_hbm, q_hbm, sum_ref, peak_ref, total_ref, prev_ref, same_ref, other_ref, out_ref, far,
+    q_ref, offsets_ref, unions, picks, counts, sem,
     *, group, heads, per_dev, owners,
 ):
     rank = lax.axis_index("ctx")
-    vper, union = picks.shape[2], unions.shape[2]
+    vper, union = picks.shape[1], unions.shape[1]
     hops = owners // 2 - 1
     slots = [(None, 0, j) for j in range(vper)]
     slots += [(k, side, j) for k in range(hops) for side in range(2) for j in range(vper)]
     extra = len(slots) % 2
     slots += [slots[-1]] * extra
+    width = heads * HEAD_SIZE
+    load = pltpu.make_async_copy(q_hbm.at[:, pl.ds(group * width, width)], q_ref, sem.at[4])
+    load.start()
+    tables = [(offsets_hbm, offsets_ref), (unions_hbm, unions), (picks_hbm, picks), (counts_hbm, counts)]
+    tables = [pltpu.make_async_copy(a, b, sem.at[i]) for i, (a, b) in enumerate(tables)]
+    for copy in tables:
+        copy.start()
     lane = lax.broadcasted_iota(jnp.int32, (1, PAIR), 1)
     block_row = lax.broadcasted_iota(jnp.int32, (per_dev, PAIR), 0)
 
+    for copy in tables:
+        copy.wait()
     hides = []
     for i in range(heads):
         head = group * heads + i
@@ -180,11 +226,11 @@
                 good = good & False
             if k is None:
                 source = prev_ref
-                block = unions[group, owner, entry]
+                block = unions[group, entry, owner]
                 distance = block_row + (per_dev - block)
                 seen = jnp.full((per_dev, PAIR), 1.0)
-                for s in range(offsets_ref.shape[1]):
-                    seen = jnp.where(distance == offsets_ref[head, s], 0.0, seen)
+                for s in range(offsets_ref.shape[0]):
+                    seen = jnp.where(distance == offsets_ref[s, head], 0.0, seen)
                 bias = jnp.where(seen * jnp.where(good, 1.0, 0.0) > 0.5, 0.0, HIDE)
                 start = block * BLOCK
             else:
@@ -209,6 +255,7 @@
             preferred_element_type=jnp.float32,
         )
 
+    load.wait()
     ahead = scores_of(0)
     for i in range(heads):
         cols = slice(i * HEAD_SIZE, (i + 1) * HEAD_SIZE)
@@ -232,23 +279,25 @@
 def attend_far(scalars, queries, sums, peaks, totals, prev, same, other, group, heads, owners):
     tokens = queries.shape[0]
     cols = heads * HEAD_SIZE
-    slots = (owners - 1) * scalars[2].shape[2]
+    slots = (owners - 1) * scalars[2].shape[1]
     slots += slots % 2
     per_dev = tokens // BLOCK
     return pl.pallas_call(
         functools.partial(far_body, group=group, heads=heads, per_dev=per_dev, owners=owners),
-        grid=(1,),
         out_shape=jax.ShapeDtypeStruct((tokens, cols), queries.dtype),
-        in_specs=[smem()] * 4 + [pl.BlockSpec((tokens, cols), lambda p: (0, group))] + [vmem()] * 6,
+        in_specs=[hbm()] * 5 + [vmem()] * 6,
         out_specs=vmem(),
         scratch_shapes=[
             pltpu.VMEM((heads, slots * BLOCK, 2 * HEAD_SIZE), queries.dtype),
+            pltpu.VMEM((tokens, cols), queries.dtype),
+            *small(scalars),
+            pltpu.SemaphoreType.DMA((5,)),
         ],
         compiler_params=pltpu.CompilerParams(vmem_limit_bytes=24 << 20),
         cost_estimate=pl.CostEstimate(
             flops=4 * tokens * cols * 512 * 3, transcendentals=tokens * heads * 512, bytes_accessed=4 * tokens * cols
         ),
-    )(*scalars, queries, sums, peaks, totals, prev, same, other)
+    )(*[stay(a) for a in scalars], stay(queries), sums, peaks, totals, prev, same, other)
 
 
 def project_body(*refs, spots, has_sum, groups):
@@ -303,24 +352,27 @@
     groups = key_rows.shape[1] // HEAD_SIZE
     owners, members = lax.axis_size("ctx"), lax.axis_size("head")
     heads = slash_offsets.shape[0] // groups
-    scalars = (slash_offsets, union_blocks, head_picks, owner_counts)
-    made = prep(union_blocks, key_rows, value_rows, groups, union_blocks.shape[2])
-    joined, blocks = made[:groups], made[groups]
+    unions = jnp.transpose(union_blocks, (0, 2, 1))
+    picks = jnp.transpose(head_picks, (0, 2, 1))
+    scalars = (slash_offsets.T, unions, picks, owner_counts)
+    made = prep(unions, key_rows, value_rows, groups, union_blocks.shape[2])
+    joined, blocks, both = made[:groups], made[groups : 2 * groups], made[2 * groups]
     hops = owners // 2 - 1
     prevs, near, sames, others = [], [], [], []
-    arrived = []
-    for k in reversed(range(hops)):
-        arrived.append(onward(blocks, "ctx", 2 * (k + 1)))
-    span = blocks.shape[0] // groups
+    if hops > 0:
+        longest = onward(both, "ctx", 2 * hops)
     for g in range(groups):
-        rows = slice(g * span, (g + 1) * span)
+        span = blocks[g].shape[0]
+        arrived = [longest[g * span : (g + 1) * span]] if hops > 0 else []
+        for k in reversed(range(hops - 1)):
+            arrived.append(onward(blocks[g], "ctx", 2 * (k + 1)))
         prevs.append(onward(joined[g], "ctx", 1))
         if hops > 0:
-            sames.append(jnp.concatenate([part[rows] for part in arrived[::-1]], axis=0))
+            sames.append(jnp.concatenate(arrived[::-1], axis=0))
             others.append(swap(sames[g], "ctx"))
         else:
-            sames.append(blocks[rows])
-            others.append(blocks[rows])
+            sames.append(blocks[g])
+            others.append(blocks[g])
     for g in range(groups):
         near.append(attend_near(scalars, queries, prevs[g], joined[g], g, heads))
     done, mates = [], []

time: 70.4 us -> 68.9 us (0.979)
  the two profiles are of different devices: /device:TPU:21 before, /device:TPU:17 now
where the time goes in v2:
time: 68.9 us; the launch traced here: 68.5 us
  starting transfers between devices  27 us (39%)
  waiting for transfers between devices  20.8 us (30%)
  Pallas kernels  20.5 us (30%)
    ppermute x7, starting transfers between devices, onward(): return lax.ppermute(array, axis, [(i, i + by) for i in range(size - by)])  14.4 us
    ppermute x2, waiting for transfers between devices, turn(): lax.ppermute(array, axis, [(i, (i + by) % size) for i in range(size)])  11.6 us
    ppermute x6, starting transfers between devices, swap(): return lax.ppermute(array, axis, [(i, i ^ 1) for i in range(size)])  10.2 us
    ppermute x7, waiting for transfers between devices, onward(): return lax.ppermute(array, axis, [(i, i + by) for i in range(size - by)])  9.18 us
    pallas_call x2, Pallas kernels, attend_near(): pl.pallas_call(functools.partial(near_body, group=group, heads=heads, per...  6.79 us
    pallas_call x6, Pallas kernels, project(): pl.pallas_call(functools.partial(project_body, spots=spots, has_sum=sums...  6.39 us
    pallas_call x2, Pallas kernels, attend_far(): pl.pallas_call(functools.partial(far_body, group=group, heads=heads, per_...  6.12 us
    ppermute x2, starting transfers between devices, turn(): lax.ppermute(array, axis, [(i, (i + by) % size) for i in range(size)])  2.37 us
  transfers between devices with their start and end apart: 15, of which 4 were waited for; matrix products, arithmetic and copies ran while one was open for 0% of the time, Pallas kernels for 26%

profile of v2, /device:TPU:17, one launch (start us, length us, event | category | flops | bytes accessed | tf_op | source)
XLA Modules:
  0.0 68.5 jit_solution(11707479719370326570)
XLA Ops:
  0.0 1.2 %prep.1 = (bf16[512,256]{1,0:T(8,128)(2,1)S(1)}, bf16[512,256]{1,0:T(8,128)(2,1)S(1)}, bf16[128,256]{1,0:T(8,128)(2,1)S(1)}, bf16[128,256]{1,0:T(8,128)(2,1)S(1)}, bf16[256,256]{1,0:T(8,128)(2,1)S(1)}) custom-call(s32[2,2,8]{2,1,0:T(2,128)} %bitcast.7, bf16[512,256]{1,0:T(8,128)(2,1)} %keys_hbm.1, bf16[512,256]{1,0:T(8,128)(2,1)} %values_hbm.1), custom_call_target="tpu_custom_call" | custom-call | tf_op jit(solution)/shard_map/prep/pallas_call | solution.py:65
  1.2 0.7 collective-permute-start.3
  1.9 3.8 %collective-permute-start.8 = (bf16[128,256]{1,0:T(8,128)(2,1)S(1)}, bf16[128,256]{1,0:T(8,128)(2,1)S(1)}, u32[]{:S(2)}, u32[]{:S(2)}) collective-permute-start(bf16[128,256]{1,0:T(8,128)(2,1)S(1)} %get-tuple-element.26), channel_id=1, source_target_pairs={{0,8},{4,12},{8,16},{12,20},{16,24},{20,28},{1,9},{5,13},{9,17},{1... | collective-permute-start | bytes 196616 | tf_op jit(solution)/shard_map/ppermute | solution.py:341
  5.7 1.3 %collective-permute-start.9 = (bf16[128,256]{1,0:T(8,128)(2,1)S(1)}, bf16[128,256]{1,0:T(8,128)(2,1)S(1)}, u32[]{:S(2)}, u32[]{:S(2)}) collective-permute-start(bf16[128,256]{1,0:T(8,128)(2,1)S(1)} %get-tuple-element.26), channel_id=1, source_target_pairs={{0,16},{4,20},{8,24},{12,28},{1,17},{5,21},{9,25},{13,29},{2,18},{... | collective-permute-start | bytes 196616 | tf_op jit(solution)/shard_map/ppermute | solution.py:341
  7.0 1.9 %collective-permute-start.1 = (bf16[128,256]{1,0:T(8,128)(2,1)S(1)}, bf16[128,256]{1,0:T(8,128)(2,1)S(1)}, u32[]{:S(2)}, u32[]{:S(2)}) collective-permute-start(bf16[128,256]{1,0:T(8,128)(2,1)S(1)} %get-tuple-element.20), channel_id=1, source_target_pairs={{0,8},{4,12},{8,16},{12,20},{16,24},{20,28},{1,9},{5,13},{9,17},{1... | collective-permute-start | bytes 196616 | tf_op jit(solution)/shard_map/ppermute | solution.py:341
  8.9 1.3 %collective-permute-start.2 = (bf16[128,256]{1,0:T(8,128)(2,1)S(1)}, bf16[128,256]{1,0:T(8,128)(2,1)S(1)}, u32[]{:S(2)}, u32[]{:S(2)}) collective-permute-start(bf16[128,256]{1,0:T(8,128)(2,1)S(1)} %get-tuple-element.20), channel_id=1, source_target_pairs={{0,16},{4,20},{8,24},{12,28},{1,17},{5,21},{9,25},{13,29},{2,18},{... | collective-permute-start | bytes 196616 | tf_op jit(solution)/shard_map/ppermute | solution.py:341
  10.2 0.0 collective-permute-done.3
  10.2 3.1 %collective-permute-start.7 = (bf16[512,256]{1,0:T(8,128)(2,1)S(1)}, bf16[512,256]{1,0:T(8,128)(2,1)S(1)}, u32[]{:S(2)}, u32[]{:S(2)}) collective-permute-start(bf16[512,256]{1,0:T(8,128)(2,1)S(1)} %get-tuple-element.22.local_ref), channel_id=1, source_target_pairs={{0,4},{4,8},{8,12},{12,16},{16,20},{20,24},{24,28},{1,5},{5,9},{9,... | collective-permute-start | bytes 786440 | tf_op jit(solution)/shard_map/ppermute | solution.py:341
  13.4 0.0 collective-permute-done.8
  13.4 2.3 %collective-permute-start = (bf16[512,256]{1,0:T(8,128)(2,1)S(1)}, bf16[512,256]{1,0:T(8,128)(2,1)S(1)}, u32[]{:S(2)}, u32[]{:S(2)}) collective-permute-start(bf16[512,256]{1,0:T(8,128)(2,1)S(1)} %get-tuple-element.16.local_ref), channel_id=1, source_target_pairs={{0,4},{4,8},{8,12},{12,16},{16,20},{20,24},{24,28},{1,5},{5,9},{9,... | collective-permute-start | bytes 786440 | tf_op jit(solution)/shard_map/ppermute | solution.py:341
  15.7 0.0 collective-permute-done.9
  15.7 1.3 %collective-permute-start.10 = (bf16[384,256]{1,0:T(8,128)(2,1)S(1)}, bf16[384,256]{1,0:T(8,128)(2,1)S(1)}, u32[]{:S(2)}, u32[]{:S(2)}) collective-permute-start(bf16[384,256]{1,0:T(8,128)(2,1)S(1)} %pad_maximum_fusion.1.same_ref), channel_id=1, source_target_pairs={{0,4},{4,0},{8,12},{12,8},{16,20},{20,16},{24,28},{28,24},{1,5},{5... | collective-permute-start | bytes 589832 | tf_op jit(solution)/shard_map/ppermute | solution.py:346
  17.0 0.0 collective-permute-done.1
  17.0 0.0 collective-permute-done.2
  17.0 0.3 collective-permute-start.4
  17.3 6.9 %collective-permute-done.7.prev_ref = bf16[512,256]{1,0:T(8,128)(2,1)S(1)} collective-permute-done((bf16[512,256]{1,0:T(8,128)(2,1)S(1)}, bf16[512,256]{1,0:T(8,128)(2,1)S(1)}, u32[]{:S(2)}, u32[]{:S(2)}) %collective-permute-start.7) | collective-permute-done | bytes 262176 | tf_op jit(solution)/shard_map/ppermute | solution.py:341
  24.2 3.3 %shard_map.84 = (f32[512,512]{1,0:T(8,128)S(1)}, f32[512,512]{1,0:T(8,128)S(1)}, f32[512,512]{1,0:T(8,128)S(1)}) custom-call(s32[4,8]{1,0:T(4,128)} %bitcast.16, s32[2,2,8]{2,1,0:T(2,128)} %bitcast.8, s32[8,1,8]{2,1,0:T(1,128)} %bitcast.12, s32[8,8]{1,0:T(8,128)} %counts_hbm.7, bf16[512,1024]{1,0:T(8,128)(2,1)} %q_hbm.7, ...), custom_call_target="tpu_custom_call" | custom-call | flops 2013265920 | bytes 1048576 | tf_op jit(solution)/shard_map/pallas_call | solution.py:172
  27.6 2.3 %collective-permute-done.prev_ref = bf16[512,256]{1,0:T(8,128)(2,1)S(1)} collective-permute-done((bf16[512,256]{1,0:T(8,128)(2,1)S(1)}, bf16[512,256]{1,0:T(8,128)(2,1)S(1)}, u32[]{:S(2)}, u32[]{:S(2)}) %collective-permute-start) | collective-permute-done | bytes 262176 | tf_op jit(solution)/shard_map/ppermute | solution.py:341
  29.8 0.0 slice-start
  29.8 3.5 %shard_map.82 = (f32[512,512]{1,0:T(8,128)S(1)}, f32[512,512]{1,0:T(8,128)S(1)}, f32[512,512]{1,0:T(8,128)S(1)}) custom-call(s32[4,8]{1,0:T(4,128)} %bitcast.17, s32[2,2,8]{2,1,0:T(2,128)} %bitcast.9, s32[8,1,8]{2,1,0:T(1,128)} %bitcast.13, s32[8,8]{1,0:T(8,128)} %counts_hbm.7, bf16[512,1024]{1,0:T(8,128)(2,1)} %q_hbm.7, ...), custom_call_target="tpu_custom_call" | custom-call | flops 2013265920 | bytes 1048576 | tf_op jit(solution)/shard_map/pallas_call | solution.py:172
  33.3 0.0 collective-permute-done.10.other_ref
  33.3 0.0 slice-start.1
  33.3 3.1 %shard_map.85.refs_0_ = bf16[512,512]{1,0:T(8,128)(2,1)S(1)} custom-call(s32[4,8]{1,0:T(4,128)} %bitcast.18, s32[2,2,8]{2,1,0:T(2,128)} %bitcast.10, s32[8,1,8]{2,1,0:T(1,128)} %bitcast.14, s32[8,8]{1,0:T(8,128)} %counts_hbm.7, bf16[512,1024]{1,0:T(8,128)(2,1)} %q_hbm.7, f32[512,512]{1,0:T(8,128)S(1)} %get-tuple-element.23.sum_ref, ...), custom_call_target="tpu_custom_call" | custom-call | flops 1610612736 | bytes 1048576 | tf_op jit(solution)/shard_map/pallas_call | solution.py:285
  36.4 1.3 %collective-permute-start.11 = (bf16[512,512]{1,0:T(8,128)(2,1)S(1)}, bf16[512,512]{1,0:T(8,128)(2,1)S(1)}, u32[]{:S(2)}, u32[]{:S(2)}) collective-permute-start(bf16[512,512]{1,0:T(8,128)(2,1)S(1)} %shard_map.85.refs_0_), channel_id=1, source_target_pairs={{0,2},{1,3},{2,0},{3,1},{4,6},{5,7},{6,4},{7,5},{8,10},{9,11},{10,... | collective-permute-start | bytes 1572872 | tf_op jit(solution)/shard_map/ppermute | solution.py:336
  37.7 0.0 collective-permute-done.4.other_ref
  37.7 3.0 %shard_map.83.refs_0_ = bf16[512,512]{1,0:T(8,128)(2,1)S(1)} custom-call(s32[4,8]{1,0:T(4,128)} %bitcast.19, s32[2,2,8]{2,1,0:T(2,128)} %bitcast.11, s32[8,1,8]{2,1,0:T(1,128)} %bitcast.15, s32[8,8]{1,0:T(8,128)} %counts_hbm.7, bf16[512,1024]{1,0:T(8,128)(2,1)} %q_hbm.7, f32[512,512]{1,0:T(8,128)S(1)} %get-tuple-element.17.sum_ref, ...), custom_call_target="tpu_custom_call" | custom-call | flops 1610612736 | bytes 1048576 | tf_op jit(solution)/shard_map/pallas_call | solution.py:285
  40.8 1.1 %collective-permute-start.5 = (bf16[512,512]{1,0:T(8,128)(2,1)S(1)}, bf16[512,512]{1,0:T(8,128)(2,1)S(1)}, u32[]{:S(2)}, u32[]{:S(2)}) collective-permute-start(bf16[512,512]{1,0:T(8,128)(2,1)S(1)} %shard_map.83.refs_0_), channel_id=1, source_target_pairs={{0,2},{1,3},{2,0},{3,1},{4,6},{5,7},{6,4},{7,5},{8,10},{9,11},{10,... | collective-permute-start | bytes 1572872 | tf_op jit(solution)/shard_map/ppermute | solution.py:336
  41.8 1.5 %collective-permute-start.14 = (bf16[512,512]{1,0:T(8,128)(2,1)S(1)}, bf16[512,512]{1,0:T(8,128)(2,1)S(1)}, u32[]{:S(2)}, u32[]{:S(2)}) collective-permute-start(bf16[512,512]{1,0:T(8,128)(2,1)S(1)} %shard_map.85.refs_0_), channel_id=1, source_target_pairs={{0,1},{1,0},{2,3},{3,2},{4,5},{5,4},{6,7},{7,6},{8,9},{9,8},{10,11... | collective-permute-start | bytes 1572872 | tf_op jit(solution)/shard_map/ppermute | solution.py:346
  43.3 0.0 collective-permute-start.13
  43.3 5.0 %collective-permute-done.11.refs_0_ = bf16[512,512]{1,0:T(8,128)(2,1)S(1)} collective-permute-done((bf16[512,512]{1,0:T(8,128)(2,1)S(1)}, bf16[512,512]{1,0:T(8,128)(2,1)S(1)}, u32[]{:S(2)}, u32[]{:S(2)}) %collective-permute-start.11) | collective-permute-done | bytes 524320 | tf_op jit(solution)/shard_map/ppermute | solution.py:336
  48.3 4.6 %collective-permute-start.12 = (bf16[512,512]{1,0:T(8,128)(2,1)S(1)}, bf16[512,512]{1,0:T(8,128)(2,1)S(1)}, u32[]{:S(2)}, u32[]{:S(2)}) collective-permute-start(bf16[512,512]{1,0:T(8,128)(2,1)S(1)} %collective-permute-done.11.refs_0_), channel_id=1, source_target_pairs={{0,1},{1,0},{2,3},{3,2},{4,5},{5,4},{6,7},{7,6},{8,9},{9,8},{10,11... | collective-permute-start | bytes 1572872 | tf_op jit(solution)/shard_map/ppermute | solution.py:346
  53.0 6.6 %collective-permute-done.5.refs_0_ = bf16[512,512]{1,0:T(8,128)(2,1)S(1)} collective-permute-done((bf16[512,512]{1,0:T(8,128)(2,1)S(1)}, bf16[512,512]{1,0:T(8,128)(2,1)S(1)}, u32[]{:S(2)}, u32[]{:S(2)}) %collective-permute-start.5) | collective-permute-done | bytes 524320 | tf_op jit(solution)/shard_map/ppermute | solution.py:336
  59.6 2.5 %collective-permute-start.6 = (bf16[512,512]{1,0:T(8,128)(2,1)S(1)}, bf16[512,512]{1,0:T(8,128)(2,1)S(1)}, u32[]{:S(2)}, u32[]{:S(2)}) collective-permute-start(bf16[512,512]{1,0:T(8,128)(2,1)S(1)} %collective-permute-done.5.refs_0_), channel_id=1, source_target_pairs={{0,1},{1,0},{2,3},{3,2},{4,5},{5,4},{6,7},{7,6},{8,9},{9,8},{10,11... | collective-permute-start | bytes 1572872 | tf_op jit(solution)/shard_map/ppermute | solution.py:346
  62.1 0.0 collective-permute-done.14.refs_1_
  62.1 0.0 slice-done
  62.1 0.0 slice-done.1
  62.1 1.3 %shard_map.86.refs_3_ = f32[512,1024]{1,0:T(8,128)S(1)} custom-call(bf16[512,512]{1,0:T(8,128)(2,1)S(1)} %shard_map.85.refs_0_, bf16[512,512]{1,0:T(8,128)(2,1)S(1)} %collective-permute-done.14.refs_1_, bf16[4096,1024]{1,0:T(8,128)(2,1)S(1)} %bitcast.6), custom_call_target="tpu_custom_call" | custom-call | flops 2147483648 | bytes 2097152 | tf_op jit(solution)/shard_map/pallas_call | solution.py:322
  63.4 0.0 collective-permute-done.13.refs_1_
  63.4 1.3 %shard_map.87.refs_2_ = f32[512,1024]{1,0:T(8,128)S(1)} custom-call(bf16[512,512]{1,0:T(8,128)(2,1)S(1)} %shard_map.83.refs_0_, bf16[512,512]{1,0:T(8,128)(2,1)S(1)} %collective-permute-done.13.refs_1_, bf16[4096,1024]{1,0:T(8,128)(2,1)S(1)} %bitcast.6, f32[512,1024]{1,0:T(8,128)S(1)} %shard_map.86.refs_3_), custom_call_target="tpu_custom_call" | custom-call | flops 2147483648 | bytes 2097152 | tf_op jit(solution)/shard_map/pallas_call | solution.py:322
  64.6 0.7 %shard_map.88.refs_2_ = f32[512,1024]{1,0:T(8,128)S(1)} custom-call(bf16[512,512]{1,0:T(8,128)(2,1)S(1)} %collective-permute-done.11.refs_0_, bf16[4096,1024]{1,0:T(8,128)(2,1)S(1)} %bitcast.6, f32[512,1024]{1,0:T(8,128)S(1)} %shard_map.87.refs_2_), custom_call_target="tpu_custom_call" | custom-call | flops 1073741824 | bytes 1048576 | tf_op jit(solution)/shard_map/pallas_call | solution.py:322
  65.4 0.0 collective-permute-done.12.refs_0_
  65.4 0.7 %shard_map.89.refs_2_ = f32[512,1024]{1,0:T(8,128)S(1)} custom-call(bf16[512,512]{1,0:T(8,128)(2,1)S(1)} %collective-permute-done.12.refs_0_, bf16[4096,1024]{1,0:T(8,128)(2,1)S(1)} %bitcast.6, f32[512,1024]{1,0:T(8,128)S(1)} %shard_map.88.refs_2_), custom_call_target="tpu_custom_call" | custom-call | flops 1073741824 | bytes 1048576 | tf_op jit(solution)/shard_map/pallas_call | solution.py:322
  66.1 0.7 %shard_map.90.refs_2_ = f32[512,1024]{1,0:T(8,128)S(1)} custom-call(bf16[512,512]{1,0:T(8,128)(2,1)S(1)} %collective-permute-done.5.refs_0_, bf16[4096,1024]{1,0:T(8,128)(2,1)S(1)} %bitcast.6, f32[512,1024]{1,0:T(8,128)S(1)} %shard_map.89.refs_2_), custom_call_target="tpu_custom_call" | custom-call | flops 1073741824 | bytes 1048576 | tf_op jit(solution)/shard_map/pallas_call | solution.py:322
  66.8 0.0 collective-permute-done.6.refs_0_
  66.8 1.7 %shard_map.91 = bf16[512,1024]{1,0:T(8,128)(2,1)} custom-call(bf16[512,512]{1,0:T(8,128)(2,1)S(1)} %collective-permute-done.6.refs_0_, bf16[4096,1024]{1,0:T(8,128)(2,1)S(1)} %bitcast.6, f32[512,1024]{1,0:T(8,128)S(1)} %shard_map.90.refs_2_), custom_call_target="tpu_custom_call" | custom-call | flops 1073741824 | bytes 1048576 | tf_op jit(solution)/shard_map/pallas_call | solution.py:322
  (4 shorter events, 0.0 us)
Async XLA Ops:
  1.2 9.0 %collective-permute-start.3 = (bf16[256,256]{1,0:T(8,128)(2,1)S(1)}, bf16[256,256]{1,0:T(8,128)(2,1)S(1)}, u32[]{:S(2)}, u32[]{:S(2)}) collective-permute-start(bf16[256,256]{1,0:T(8,128)(2,1)S(1)} %get-tuple-element.21), channel_id=1, source_target_pairs={{0,24},{4,28},{1,25},{5,29},{2,26},{6,30},{3,27},{7,31}} | collective-permute-start | bytes 393224 | tf_op jit(solution)/shard_map/ppermute | solution.py:341
  1.9 11.5 %collective-permute-start.8 = (bf16[128,256]{1,0:T(8,128)(2,1)S(1)}, bf16[128,256]{1,0:T(8,128)(2,1)S(1)}, u32[]{:S(2)}, u32[]{:S(2)}) collective-permute-start(bf16[128,256]{1,0:T(8,128)(2,1)S(1)} %get-tuple-element.26), channel_id=1, source_target_pairs={{0,8},{4,12},{8,16},{12,20},{16,24},{20,28},{1,9},{5,13},{9,17},{1... | collective-permute-start | bytes 196616 | tf_op jit(solution)/shard_map/ppermute | solution.py:341
  5.7 10.0 %collective-permute-start.9 = (bf16[128,256]{1,0:T(8,128)(2,1)S(1)}, bf16[128,256]{1,0:T(8,128)(2,1)S(1)}, u32[]{:S(2)}, u32[]{:S(2)}) collective-permute-start(bf16[128,256]{1,0:T(8,128)(2,1)S(1)} %get-tuple-element.26), channel_id=1, source_target_pairs={{0,16},{4,20},{8,24},{12,28},{1,17},{5,21},{9,25},{13,29},{2,18},{... | collective-permute-start | bytes 196616 | tf_op jit(solution)/shard_map/ppermute | solution.py:341
  7.0 10.0 %collective-permute-start.1 = (bf16[128,256]{1,0:T(8,128)(2,1)S(1)}, bf16[128,256]{1,0:T(8,128)(2,1)S(1)}, u32[]{:S(2)}, u32[]{:S(2)}) collective-permute-start(bf16[128,256]{1,0:T(8,128)(2,1)S(1)} %get-tuple-element.20), channel_id=1, source_target_pairs={{0,8},{4,12},{8,16},{12,20},{16,24},{20,28},{1,9},{5,13},{9,17},{1... | collective-permute-start | bytes 196616 | tf_op jit(solution)/shard_map/ppermute | solution.py:341
  8.9 8.1 %collective-permute-start.2 = (bf16[128,256]{1,0:T(8,128)(2,1)S(1)}, bf16[128,256]{1,0:T(8,128)(2,1)S(1)}, u32[]{:S(2)}, u32[]{:S(2)}) collective-permute-start(bf16[128,256]{1,0:T(8,128)(2,1)S(1)} %get-tuple-element.20), channel_id=1, source_target_pairs={{0,16},{4,20},{8,24},{12,28},{1,17},{5,21},{9,25},{13,29},{2,18},{... | collective-permute-start | bytes 196616 | tf_op jit(solution)/shard_map/ppermute | solution.py:341
  10.2 14.0 %collective-permute-start.7 = (bf16[512,256]{1,0:T(8,128)(2,1)S(1)}, bf16[512,256]{1,0:T(8,128)(2,1)S(1)}, u32[]{:S(2)}, u32[]{:S(2)}) collective-permute-start(bf16[512,256]{1,0:T(8,128)(2,1)S(1)} %get-tuple-element.22.local_ref), channel_id=1, source_target_pairs={{0,4},{4,8},{8,12},{12,16},{16,20},{20,24},{24,28},{1,5},{5,9},{9,... | collective-permute-start | bytes 786440 | tf_op jit(solution)/shard_map/ppermute | solution.py:341
  13.4 16.4 %collective-permute-start = (bf16[512,256]{1,0:T(8,128)(2,1)S(1)}, bf16[512,256]{1,0:T(8,128)(2,1)S(1)}, u32[]{:S(2)}, u32[]{:S(2)}) collective-permute-start(bf16[512,256]{1,0:T(8,128)(2,1)S(1)} %get-tuple-element.16.local_ref), channel_id=1, source_target_pairs={{0,4},{4,8},{8,12},{12,16},{16,20},{20,24},{24,28},{1,5},{5,9},{9,... | collective-permute-start | bytes 786440 | tf_op jit(solution)/shard_map/ppermute | solution.py:341
  15.7 17.6 %collective-permute-start.10 = (bf16[384,256]{1,0:T(8,128)(2,1)S(1)}, bf16[384,256]{1,0:T(8,128)(2,1)S(1)}, u32[]{:S(2)}, u32[]{:S(2)}) collective-permute-start(bf16[384,256]{1,0:T(8,128)(2,1)S(1)} %pad_maximum_fusion.1.same_ref), channel_id=1, source_target_pairs={{0,4},{4,0},{8,12},{12,8},{16,20},{20,16},{24,28},{28,24},{1,5},{5... | collective-permute-start | bytes 589832 | tf_op jit(solution)/shard_map/ppermute | solution.py:346
  17.0 20.7 %collective-permute-start.4 = (bf16[384,256]{1,0:T(8,128)(2,1)S(1)}, bf16[384,256]{1,0:T(8,128)(2,1)S(1)}, u32[]{:S(2)}, u32[]{:S(2)}) collective-permute-start(bf16[384,256]{1,0:T(8,128)(2,1)S(1)} %pad_maximum_fusion.same_ref), channel_id=1, source_target_pairs={{0,4},{4,0},{8,12},{12,8},{16,20},{20,16},{24,28},{28,24},{1,5},{5... | collective-permute-start | bytes 589832 | tf_op jit(solution)/shard_map/ppermute | solution.py:346
  29.8 32.2 %slice-start = ((s8[8388608]{0:T(1024)(128)(4,1)}), s8[4194304]{0:T(1024)(128)(4,1)S(1)}, s32[]{:S(2)}) async-start(s8[8388608]{0:T(1024)(128)(4,1)} %bitcast.5), calls=%async_computation | async-start | bytes 8388608
  33.3 28.8 %slice-start.1 = ((s8[8388608]{0:T(1024)(128)(4,1)}), s8[4194304]{0:T(1024)(128)(4,1)S(1)}, s32[]{:S(2)}) async-start(s8[8388608]{0:T(1024)(128)(4,1)} %bitcast.5), calls=%async_computation.1 | async-start | bytes 8388608
  36.4 11.9 %collective-permute-start.11 = (bf16[512,512]{1,0:T(8,128)(2,1)S(1)}, bf16[512,512]{1,0:T(8,128)(2,1)S(1)}, u32[]{:S(2)}, u32[]{:S(2)}) collective-permute-start(bf16[512,512]{1,0:T(8,128)(2,1)S(1)} %shard_map.85.refs_0_), channel_id=1, source_target_pairs={{0,2},{1,3},{2,0},{3,1},{4,6},{5,7},{6,4},{7,5},{8,10},{9,11},{10,... | collective-permute-start | bytes 1572872 | tf_op jit(solution)/shard_map/ppermute | solution.py:336
  40.8 18.8 %collective-permute-start.5 = (bf16[512,512]{1,0:T(8,128)(2,1)S(1)}, bf16[512,512]{1,0:T(8,128)(2,1)S(1)}, u32[]{:S(2)}, u32[]{:S(2)}) collective-permute-start(bf16[512,512]{1,0:T(8,128)(2,1)S(1)} %shard_map.83.refs_0_), channel_id=1, source_target_pairs={{0,2},{1,3},{2,0},{3,1},{4,6},{5,7},{6,4},{7,5},{8,10},{9,11},{10,... | collective-permute-start | bytes 1572872 | tf_op jit(solution)/shard_map/ppermute | solution.py:336
  41.8 20.2 %collective-permute-start.14 = (bf16[512,512]{1,0:T(8,128)(2,1)S(1)}, bf16[512,512]{1,0:T(8,128)(2,1)S(1)}, u32[]{:S(2)}, u32[]{:S(2)}) collective-permute-start(bf16[512,512]{1,0:T(8,128)(2,1)S(1)} %shard_map.85.refs_0_), channel_id=1, source_target_pairs={{0,1},{1,0},{2,3},{3,2},{4,5},{5,4},{6,7},{7,6},{8,9},{9,8},{10,11... | collective-permute-start | bytes 1572872 | tf_op jit(solution)/shard_map/ppermute | solution.py:346
  43.3 20.1 %collective-permute-start.13 = (bf16[512,512]{1,0:T(8,128)(2,1)S(1)}, bf16[512,512]{1,0:T(8,128)(2,1)S(1)}, u32[]{:S(2)}, u32[]{:S(2)}) collective-permute-start(bf16[512,512]{1,0:T(8,128)(2,1)S(1)} %shard_map.83.refs_0_), channel_id=1, source_target_pairs={{0,1},{1,0},{2,3},{3,2},{4,5},{5,4},{6,7},{7,6},{8,9},{9,8},{10,11... | collective-permute-start | bytes 1572872 | tf_op jit(solution)/shard_map/ppermute | solution.py:346
  48.3 17.1 %collective-permute-start.12 = (bf16[512,512]{1,0:T(8,128)(2,1)S(1)}, bf16[512,512]{1,0:T(8,128)(2,1)S(1)}, u32[]{:S(2)}, u32[]{:S(2)}) collective-permute-start(bf16[512,512]{1,0:T(8,128)(2,1)S(1)} %collective-permute-done.11.refs_0_), channel_id=1, source_target_pairs={{0,1},{1,0},{2,3},{3,2},{4,5},{5,4},{6,7},{7,6},{8,9},{9,8},{10,11... | collective-permute-start | bytes 1572872 | tf_op jit(solution)/shard_map/ppermute | solution.py:346
  59.6 7.3 %collective-permute-start.6 = (bf16[512,512]{1,0:T(8,128)(2,1)S(1)}, bf16[512,512]{1,0:T(8,128)(2,1)S(1)}, u32[]{:S(2)}, u32[]{:S(2)}) collective-permute-start(bf16[512,512]{1,0:T(8,128)(2,1)S(1)} %collective-permute-done.5.refs_0_), channel_id=1, source_target_pairs={{0,1},{1,0},{2,3},{3,2},{4,5},{5,4},{6,7},{7,6},{8,9},{9,8},{10,11... | collective-permute-start | bytes 1572872 | tf_op jit(solution)/shard_map/ppermute | solution.py:346
